TPU v7x, 256 devices: a whole 4x4x8 slice. The times are simulated.
256 devices in a mesh: ka: 32 (over z_hi, x, y), ga: 8 (over z_lo, core).
Axes of the slice: x: 4, y: 4, z: 8 (z_hi: 2, z_lo: 4; z = z_hi * 4 + z_lo), core: 2. Of those that a mesh axis runs over, the one named last changes fastest.
Arguments:
- psi: bfloat16 [32, 2, 128, 2048], P('ka', None, None, 'ga'), may hold values from -0.62890625 to 0.62890625
- dvscf: bfloat16 [96, 2, 2048], P(None, None, 'ga'), may hold values from -6 to 6
- kq_map: int32 [32], P('ka'), may hold values from 0 to 31, each once
Outputs:
- coupling: float32 [96, 32, 2, 128, 128], P('ga', 'ka')
Inputs may be any that keep to these rules, and one draw needn't show every extreme that they name: kq_map is a permutation of the k-points 0 to 31.
All inputs are finite; a program needn't handle non-finite values.
Results may differ from a plain program's by a relative error of at most 0.0029.
Values may be sent and summed in bfloat16 or wider, within the bound.
No kernel may reach another device: no remote copies, remote signals or barrier semaphores. Data moves between devices by JAX's collectives and lax.ppermute only.
A program may use at most 128 MiB of HBM per device.

v0:
```python
import jax
import jax.numpy as jnp
from jax import lax
from jax.sharding import Mesh
from jax.sharding import PartitionSpec as P

KA = ("ka_0", "ka_1", "ka_2")


def joined_along(blocks, dim):
    dims = list(blocks.shape[1:])
    dims[dim] *= blocks.shape[0]
    return jnp.moveaxis(blocks, 0, dim).reshape(dims)


def gather_in_order(value, axes, sequence):
    blocks = value[None]
    for k in sequence:
        blocks = lax.all_gather(blocks, axes[k], axis=0, tiled=True)
    current = [lax.axis_size(axes[k]) for k in reversed(sequence)]
    blocks = blocks.reshape(*current, *value.shape)
    turned = sorted(range(len(sequence)), key=lambda place: sequence[len(sequence) - 1 - place])
    return blocks.transpose(*turned, *range(len(sequence), blocks.ndim)).reshape(-1, *value.shape)


def gathered_by_axis(value, axes, sequence, dim):
    return joined_along(gather_in_order(value, axes, sequence), dim)


def in_one_piece(arrays, axis, dim, along):
    ends, at = ([], 0)
    for a in arrays[:-1]:
        at += a.shape[along]
        ends.append(at)
    both = jnp.concatenate(arrays, axis=along)
    return tuple(jnp.split(lax.all_gather(both, axis, axis=dim, tiled=True), ends, axis=along))


def block_modes(left, wave_real, wave_imag, potential):
    dv_real = potential[:, 0].astype(jnp.float32)[:, None, None, :]
    dv_imag = potential[:, 1].astype(jnp.float32)[:, None, None, :]
    prod_real = (dv_real * wave_real[None] - dv_imag * wave_imag[None]).astype(jnp.bfloat16)
    prod_imag = (dv_real * wave_imag[None] + dv_imag * wave_real[None]).astype(jnp.bfloat16)
    right = jnp.stack(
        [
            jnp.concatenate([prod_real, prod_imag], axis=-1),
            jnp.concatenate([prod_imag, -prod_real], axis=-1),
        ],
        axis=2,
    )
    return jnp.einsum("kmr,ukcnr->ukcmn", left, right, preferred_element_type=jnp.float32)


def mode_block(left, wave, dv_block):
    wave_real = wave[:, 0].astype(jnp.float32)
    wave_imag = wave[:, 1].astype(jnp.float32)
    return block_modes(left, wave_real, wave_imag, dv_block)


def stack_left(other):
    return jnp.concatenate([other[:, 0], other[:, 1]], axis=-1)


def body(psi, dvscf, kq_map):
    piece = gathered_by_axis(psi, KA, (0, 1, 2), 0)
    within = (kq_map >= 0) & (kq_map < piece.shape[0])
    clipped = jnp.clip(kq_map, 0, piece.shape[0] - 1)
    taken = jnp.take(piece, clipped, axis=0)
    phi = jnp.where(within[:, None, None, None], taken, jnp.zeros_like(psi))
    dv_modes = lax.all_to_all(dvscf, "ga", split_axis=0, concat_axis=2, tiled=True)
    wave_piece, other_piece = in_one_piece((psi, phi), "ga", 3, 0)
    return mode_block(stack_left(other_piece), wave_piece, dv_modes)


def solution(mesh):
    finer = Mesh(mesh.devices.reshape(2, 4, 4, mesh.shape["ga"]), ("ka_0", "ka_1", "ka_2", "ga"))
    in_specs = (P(KA, None, None, "ga"), P(None, None, "ga"), P(KA))
    out_specs = P("ga", KA, None, None, None)
    return jax.shard_map(body, mesh=finer, in_specs=in_specs, out_specs=out_specs, check_vma=False)
```

profile of v0, /device:TPU:1, one launch (start us, length us, event | category | flops | bytes accessed | tf_op | source)
XLA Modules:
  0.0 180.3 jit_solution(7627843267096762044)
XLA Ops:
  6.5 0.0 all-gather.9.cloned.1.call-start
  6.5 13.4 %all-gather = bf16[2,2,128,256]{3,2,1,0:T(8,128)(2,1)} all-gather(bf16[1,2,128,256]{3,2,1,0:T(8,128)(2,1)} %param.3), channel_id=2, replica_groups=mesh['ka_0'=2,'ka_1'=4,'ka_2'=4,'ga'=8] {'ka_0'}, dimensions={0}, use_global_device_ids=true | all-gather | bytes 393216 | tf_op jit(solution)/shard_map/all_gather | solution.py:19
  19.9 0.0 all-gather.9.cloned.1.call-update
  19.9 0.0 all-gather.11.cloned.1.call-start
  20.0 27.5 %all-gather.9.cloned.1.call-done = bf16[8,2,128,256]{3,2,1,0:T(8,128)(2,1)} async-done(((bf16[2,2,128,256]{3,2,1,0:T(8,128)(2,1)}), bf16[8,2,128,256]{3,2,1,0:T(8,128)(2,1)}) %all-gather.9.cloned.1.call-update) | async-done | bytes 1048592 | tf_op jit(solution)/shard_map/all_gather | solution.py:19
  47.5 0.0 all-gather.11.cloned.1.call-update
  47.6 0.0 all-gather.7.cloned.1.call-start
  48.3 54.2 %all-gather.11.cloned.1.call-done = bf16[32,2,128,256]{3,2,1,0:T(8,128)(2,1)} async-done(((bf16[8,2,128,256]{3,2,1,0:T(8,128)(2,1)}), bf16[32,2,128,256]{3,2,1,0:T(8,128)(2,1)}) %all-gather.11.cloned.1.call-update) | async-done | bytes 4194320 | tf_op jit(solution)/shard_map/all_gather | solution.py:19
  102.5 2.5 %copy.13 = bf16[4,4,2,1,2,128,256]{6,5,4,0,1,2,3:T(8,128)(2,1)S(1)} copy(bf16[4,4,2,1,2,128,256]{6,5,4,2,1,0,3:T(8,128)(2,1)} %bitcast.54) | data formatting | bytes 8388608 | tf_op jit(solution)/shard_map/reshape | solution.py:21
  104.9 1.6 pad_maximum_fusion
  106.6 0.0 all-gather.7.cloned.1.call-update
  106.6 11.0 %all_to_all.18 = bf16[96,2,256]{2,1,0:T(2,128)(2,1)S(1)} all-to-all(bf16[96,2,256]{2,1,0:T(2,128)(2,1)} %param.4), channel_id=1, replica_groups=mesh['ka_0'=2,'ka_1'=4,'ka_2'=4,'ga'=8] {'ga'}, dimensions={0} | all-to-all | bytes 196608 | tf_op jit(solution)/shard_map/all_to_all | solution.py:70
  117.7 0.1 slice_convert_fusion.1
  117.8 0.1 copy_bitcast_fusion
  117.9 28.4 %all-gather.7.cloned.1.call-done = bf16[2,2,128,2048]{3,2,1,0:T(8,128)(2,1)} async-done(((bf16[2,2,128,256]{3,2,1,0:T(8,128)(2,1)}), bf16[2,2,128,2048]{3,2,1,0:T(8,128)(2,1)}) %all-gather.7.cloned.1.call-update) | async-done | bytes 2097168 | tf_op jit(solution)/shard_map/all_gather | solution.py:36
  146.3 2.8 %slice_bitcast_fusion.1 = (bf16[1,128,2048]{2,1,0:T(8,128)(2,1)}, bf16[1,128,2048]{2,1,0:T(8,128)(2,1)}, f32[128,2048]{1,0:T(8,128)S(1)}, f32[128,2048]{1,0:T(8,128)S(1)}) fusion(bf16[2,2,128,2048]{3,2,1,0:T(8,128)(2,1)} %all-gather.7.cloned.1.call-done), kind=kLoop, calls=%fused_computation.13 | loop fusion | flops 524288 | bytes 5242880 | tf_op jit(solution)/shard_map/squeeze | solution.py:61
  149.1 1.9 %fusion.10 = bf16[12,1,128,2048]{3,2,0,1:T(8,128)(2,1)S(1)} fusion(f32[128,2048]{1,0:T(8,128)S(1)} %get-tuple-element.22, f32[12,2048]{1,0:T(8,128)S(1)} %get-tuple-element.26, f32[128,2048]{1,0:T(8,128)S(1)} %get-tuple-element.23, f32[12,2048]{1,0:T(8,128)S(1)} %get-tuple-element.27), kind=kLoop, calls=%fused_computation.27 | loop fusion | flops 15728640 | bytes 8585216 | tf_op jit(solution)/shard_map/neg | solution.py:47
  151.0 3.4 %subtract_convert_fusion = (bf16[12,1,128,2048]{3,2,0,1:T(8,128)(2,1)S(1)}, bf16[12,1,128,2048]{3,2,0,1:T(8,128)(2,1)S(1)}) fusion(f32[128,2048]{1,0:T(8,128)S(1)} %get-tuple-element.22, f32[12,2048]{1,0:T(8,128)S(1)} %get-tuple-element.26, f32[128,2048]{1,0:T(8,128)S(1)} %get-tuple-element.23, f32[12,2048]{1,0:T(8,128)S(1)} %get-tuple-element.27), kind=kLoop, calls=%fused_computation.7 | loop fusion | flops 25165824 | bytes 14876672 | tf_op jit(solution)/shard_map/convert_element_type | solution.py:42
  154.4 5.5 %maximum_bitcast_fusion.2 = (bf16[12,1,1,128,4096]{4,3,2,0,1:T(8,128)(2,1)S(1)}, bf16[12,1,1,128,4096]{4,3,2,0,1:T(8,128)(2,1)}) fusion(bf16[12,1,128,2048]{3,2,0,1:T(8,128)(2,1)S(1)} %get-tuple-element.19, bf16[12,1,128,2048]{3,2,0,1:T(8,128)(2,1)S(1)} %get-tuple-element.18, bf16[12,1,128,2048]{3,2,0,1:T(8,128)(2,1)S(1)} %fusion.10), kind=kLoop, calls=%fused_computation.4 | loop fusion | flops 50331648 | bytes 44040192 | tf_op jit(solution)/shard_map/stack | solution.py:44
  159.9 10.8 %fusion.3 = f32[12,1,2,128,128]{3,4,2,0,1:T(8,128)} fusion(bf16[12,1,1,128,4096]{4,3,2,0,1:T(8,128)(2,1)} %get-tuple-element.17, bf16[12,1,1,128,4096]{4,3,2,0,1:T(8,128)(2,1)S(1)} %get-tuple-element.16, bf16[1,128,2048]{2,1,0:T(8,128)(2,1)} %get-tuple-element.21, bf16[1,128,2048]{2,1,0:T(8,128)(2,1)} %get-tuple-element.20), kind=kOutput, calls=%fused_computation.8 | convolution fusion | flops 3235905536 | bytes 27787264 | tf_op jit(solution)/shard_map/kmr,ukcnr->ukcmn/dot_general | solution.py:51
  170.7 3.0 %copy.15 = f32[12,1,2,128,128]{4,3,2,1,0:T(8,128)} copy(f32[12,1,2,128,128]{3,4,2,0,1:T(8,128)} %fusion.3) | data formatting | bytes 3145728 | tf_op jit(solution)/shard_map/kmr,ukcnr->ukcmn/transpose | solution.py:51
  (3 shorter events, 0.1 us)
Async XLA Ops:
  6.5 41.0 %all-gather.9.cloned.1.call-start = ((), (), s32[]{:S(2)}) async-start(), calls=%async_computation.2 | async-start | bytes 1310720 | tf_op jit(solution)/shard_map/all_gather | solution.py:19
  19.9 82.5 %all-gather.11.cloned.1.call-start = ((), (), s32[]{:S(2)}) async-start(), calls=%async_computation.3 | async-start | bytes 5242880 | tf_op jit(solution)/shard_map/all_gather | solution.py:19
  47.6 98.7 %all-gather.7.cloned.1.call-start = ((), (), s32[]{:S(2)}) async-start(), calls=%async_computation.1 | async-start | bytes 2359296 | tf_op jit(solution)/shard_map/all_gather | solution.py:36
Sparse Core Ops, SparseCore 0:
  20.1 27.4 all-gather.8
  49.3 53.0 all-gather.10
  106.7 39.5 all-gather.6
where the time goes:
time: 181 us; the launch traced here: 180 us
  waiting for transfers between devices  110 us (61%)
  blocking collectives  24.4 us (13%)
  other arithmetic  15.4 us (9%)
  between operations  13.8 us (8%)
  matrix products  10.8 us (6%)
  local copies, waits for them, and re-layouts  5.59 us (3%)
    all_gather x2, waiting for transfers between devices, gather_in_order(): blocks = lax.all_gather(blocks, axes[k], axis=0, tiled=True)  81.7 us
    all_gather x1, waiting for transfers between devices, in_one_piece(): lax.all_gather(both, axis, axis=dim, tiled=True)  28.4 us
    all_gather x1, blocking collectives, gather_in_order(): blocks = lax.all_gather(blocks, axes[k], axis=0, tiled=True)  13.4 us
    all_to_all x1, blocking collectives, body(): lax.all_to_all(dvscf, 'ga', split_axis=0, concat_axis=2, tiled=True)  11 us
    dot_general x1, matrix products, block_modes(): jnp.einsum('kmr,ukcnr->ukcmn', left, right, preferred_element_type=jnp.fl...  10.8 us
    another operation x1, other arithmetic, block_modes(): jnp.stack([jnp.concatenate([prod_real, prod_imag], axis=-1), jnp.concaten...  5.48 us
  transfers between devices with their start and end apart: 3, of which 3 were waited for; matrix products, arithmetic and copies ran while one was open for 0% of the time, Pallas kernels for 0%

commit v1 on v0

v1 whole, which is shorter than its diff:
```python
import jax
import jax.numpy as jnp
from jax import lax
from jax.experimental import pallas as pl
from jax.experimental.pallas import tpu as pltpu
from jax.sharding import Mesh
from jax.sharding import PartitionSpec as P

KA = ("zh", "x", "y")
GA = ("zl", "c")
SWAP = [(0, 1), (1, 0)]


def ring(step, size=4):
    return [(i, (i + step) % size) for i in range(size)]


def couple(half, waves, others, potentials, modes):
    parts = len(waves)
    bands, cells = waves[0].shape[0] // 2, waves[0].shape[1]
    wide = parts * cells

    def kernel(half_ref, *refs):
        wave_refs, other_refs, pot_refs = refs[:parts], refs[parts : 2 * parts], refs[2 * parts : 3 * parts]
        out_ref = refs[3 * parts]
        wave_re, wave_im, left, right_a, right_b = refs[3 * parts + 1 :]
        step = pl.program_id(0)
        first = half_ref[0] * modes

        def fill(mode, right):
            for p in range(parts):
                at = slice(p * cells, (p + 1) * cells)
                dv_re = pot_refs[p][mode, 0:1, :].astype(jnp.float32)
                dv_im = pot_refs[p][mode, 1:2, :].astype(jnp.float32)
                w_re, w_im = wave_re[:, at], wave_im[:, at]
                right[:bands, at] = (dv_re * w_re - dv_im * w_im).astype(jnp.bfloat16)
                right[bands:, at] = (dv_re * w_im + dv_im * w_re).astype(jnp.bfloat16)

        def finish(slot, right):
            full = lax.dot_general(left[...], right[...], (((1,), (1,)), ((), ())), preferred_element_type=jnp.float32)
            out_ref[slot, 0] = full[:bands, :bands] + full[bands:, bands:]
            out_ref[slot, 1] = full[:bands, bands:] - full[bands:, :bands]

        @pl.when(step == 0)
        def _():
            for p in range(parts):
                at = slice(p * cells, (p + 1) * cells)
                wave_re[:, at] = wave_refs[p][:bands].astype(jnp.float32)
                wave_im[:, at] = wave_refs[p][bands:].astype(jnp.float32)
                left[:, at] = other_refs[p][...]
            fill(first, right_a)

        fill(first + 2 * step + 1, right_b)
        finish(0, right_a)
        fill(first + jnp.minimum(2 * step + 2, modes - 1), right_a)
        finish(1, right_b)

    whole = lambda a: pl.BlockSpec(a.shape, lambda i: (0,) * a.ndim)
    return pl.pallas_call(
        kernel,
        grid=(modes // 2,),
        in_specs=[pl.BlockSpec(memory_space=pltpu.SMEM)] + [whole(a) for a in (*waves, *others, *potentials)],
        out_specs=pl.BlockSpec((2, 2, bands, bands), lambda i: (i, 0, 0, 0)),
        out_shape=jax.ShapeDtypeStruct((modes, 2, bands, bands), jnp.float32),
        scratch_shapes=[
            pltpu.VMEM((bands, wide), jnp.float32),
            pltpu.VMEM((bands, wide), jnp.float32),
            pltpu.VMEM((2 * bands, wide), jnp.bfloat16),
            pltpu.VMEM((2 * bands, wide), jnp.bfloat16),
            pltpu.VMEM((2 * bands, wide), jnp.bfloat16),
        ],
        compiler_params=pltpu.CompilerParams(dimension_semantics=("arbitrary",)),
    )(half, *waves, *others, *potentials)


def pick(number, choices):
    out = choices[0]
    for i, choice in enumerate(choices[1:], 1):
        out = jnp.where(number == i, choice, out)
    return out


def body(psi, dvscf, kq_map):
    zh, x, y, zl, c = (lax.axis_index(a) for a in ("zh", "x", "y", "zl", "c"))
    bands, cells = psi.shape[2], psi.shape[3]
    slab = psi.reshape(2 * bands, cells)
    chip_modes = dvscf.shape[0] // 4
    modes = chip_modes // 2

    swapped = lax.ppermute(slab, "zh", SWAP)
    near = [slab] + [lax.ppermute(slab, "y", ring(s)) for s in (1, 2, 3)]
    wanted = [kq_map] + [lax.ppermute(kq_map, "x", ring(-s)) for s in (1, 2, 3)]
    far = [swapped] + [lax.ppermute(swapped, "y", ring(s)) for s in (1, 2, 3)]
    slots = []
    for k in wanted:
        source = k[0]
        back = (y - source % 4) % 4
        slots.append(pick(jnp.where(source // 16 == zh, back, back + 4), near + far))
    came = [slots[0]] + [lax.ppermute(slots[s], "x", ring(s)) for s in (1, 2, 3)]
    phi = pick((x - (kq_map[0] // 4) % 4) % 4, came)

    slab_late, _ = lax.optimization_barrier((slab, swapped))
    waves = [slab] + [lax.ppermute(slab_late, "zl", ring(s)) for s in (1, 3, 2)]
    potentials = []
    for s in (0, 1, 3, 2):
        part = lax.dynamic_slice_in_dim(dvscf, chip_modes * ((zl + s) % 4), chip_modes, 0)
        potentials.append(lax.ppermute(part, "zl", ring(s)) if s else part)
    others = [phi] + [lax.ppermute(phi, "zl", ring(s)) for s in (1, 3, 2)]

    theirs = couple((1 - c)[None].astype(jnp.int32), waves, others, potentials, modes)
    theirs = lax.ppermute(theirs, "c", SWAP)
    mine = couple(c[None].astype(jnp.int32), waves, others, potentials, modes)
    return (mine + theirs)[:, None]


def solution(mesh):
    finer = Mesh(mesh.devices.reshape(2, 4, 4, 4, 2), KA + GA)
    in_specs = (P(KA, None, None, GA), P(None, None, GA), P(KA))
    out_specs = P(GA, KA, None, None, None)
    return jax.shard_map(body, mesh=finer, in_specs=in_specs, out_specs=out_specs, check_vma=False)
```

time: 181 us -> 87.3 us (0.48)
  waiting for transfers between devices: 110 us -> 23.4 us
  starting transfers between devices: 0.08 us -> 37 us
  blocking collectives: 24.4 us -> 0 us
  Pallas kernels: 0 us -> 11.7 us
  matrix products: 10.8 us -> 0 us
  other arithmetic: 15.4 us -> 4.78 us
  between operations: 13.8 us -> 8.8 us
  local copies, waits for them, and re-layouts: 5.59 us -> 1.29 us
    all_gather x3 -> x0, waiting for transfers between devices: 110 us -> none  [the longest x2 81.7 us: gather_in_order(): blocks = lax.all_gather(blocks, axes[k], axis=0, tiled=True)]
    ppermute x0 -> x23, starting transfers between devices: none -> 37 us  [the longest x1 7.73 us: body(): swapped = lax.ppermute(slab, 'zh', SWAP)]
    ppermute x0 -> x23, waiting for transfers between devices: none -> 23.4 us  [the longest x3 9.81 us: body(): others = [phi] + [lax.ppermute(phi, 'zl', ring(s)) for s in (1, 3, 2)]]
    all_gather x1 -> x0, blocking collectives: 13.4 us -> none  [gather_in_order(): blocks = lax.all_gather(blocks, axes[k], axis=0, tiled=True)]
    pallas_call x0 -> x2, Pallas kernels: none -> 11.7 us  [couple(): pl.pallas_call(kernel, grid=(modes // 2,), in_specs=[pl.BlockSpec(memory_...]
    all_to_all x1 -> x0, blocking collectives: 11 us -> none  [body(): lax.all_to_all(dvscf, 'ga', split_axis=0, concat_axis=2, tiled=True)]
    dot_general x1 -> x0, matrix products: 10.8 us -> none  [block_modes(): jnp.einsum('kmr,ukcnr->ukcmn', left, right, preferred_element_type=jnp.fl...]
    another operation x1 -> x0, other arithmetic: 5.48 us -> none  [block_modes(): jnp.stack([jnp.concatenate([prod_real, prod_imag], axis=-1), jnp.concaten...]
  transfers between devices with their start and end apart: 3 -> 23, of which waited for: 3 -> 5; matrix products, arithmetic and copies ran while one was open for 0% -> 2% of each run, Pallas kernels for 0% -> 7%
where the time goes in v1:
time: 87.3 us; the launch traced here: 87 us
  starting transfers between devices  37 us (42%)
  waiting for transfers between devices  23.4 us (27%)
  Pallas kernels  11.7 us (13%)
  between operations  8.8 us (10%)
  other arithmetic  4.78 us (5%)
  local copies, waits for them, and re-layouts  1.29 us (1%)
    pallas_call x2, Pallas kernels, couple(): pl.pallas_call(kernel, grid=(modes // 2,), in_specs=[pl.BlockSpec(memory_...  11.7 us
    ppermute x3, waiting for transfers between devices, body(): others = [phi] + [lax.ppermute(phi, 'zl', ring(s)) for s in (1, 3, 2)]  9.81 us
    ppermute x3, waiting for transfers between devices, body(): waves = [slab] + [lax.ppermute(slab_late, 'zl', ring(s)) for s in (1, 3, 2)]  8.56 us
    ppermute x1, starting transfers between devices, body(): swapped = lax.ppermute(slab, 'zh', SWAP)  7.73 us
    ppermute x3, starting transfers between devices, body(): wanted = [kq_map] + [lax.ppermute(kq_map, 'x', ring(-s)) for s in (1, 2, 3)]  5.46 us
    ppermute x3, waiting for transfers between devices, body(): wanted = [kq_map] + [lax.ppermute(kq_map, 'x', ring(-s)) for s in (1, 2, 3)]  5.04 us
    ppermute x3, starting transfers between devices, body(): near = [slab] + [lax.ppermute(slab, 'y', ring(s)) for s in (1, 2, 3)]  4.38 us
    ppermute x3, starting transfers between devices, body(): waves = [slab] + [lax.ppermute(slab_late, 'zl', ring(s)) for s in (1, 3, 2)]  3.89 us
  transfers between devices with their start and end apart: 23, of which 5 were waited for; matrix products, arithmetic and copies ran while one was open for 2% of the time, Pallas kernels for 7%

profile of v1, /device:TPU:1, one launch (start us, length us, event | category | flops | bytes accessed | tf_op | source)
XLA Modules:
  0.0 87.0 jit_solution(18415598289040670663)
XLA Ops:
  0.0 7.7 %collective-permute-start = (bf16[256,256]{1,0:T(8,128)(2,1)}, bf16[256,256]{1,0:T(8,128)(2,1)S(1)}, u32[]{:S(2)}, u32[]{:S(2)}) collective-permute-start(bf16[256,256]{1,0:T(8,128)(2,1)} %bitcast.19), channel_id=1, source_target_pairs={{0,128},{128,0},{1,129},{129,1},{2,130},{130,2},{3,131},{131,3},{4... | collective-permute-start | bytes 393224 | tf_op jit(solution)/shard_map/ppermute | solution.py:90
  7.7 1.3 %collective-permute-start.10 = (bf16[256,256]{1,0:T(8,128)(2,1)}, bf16[256,256]{1,0:T(8,128)(2,1)S(1)}, u32[]{:S(2)}, u32[]{:S(2)}) collective-permute-start(bf16[256,256]{1,0:T(8,128)(2,1)} %bitcast.20), channel_id=1, source_target_pairs={{0,8},{8,16},{16,24},{24,0},{1,9},{9,17},{17,25},{25,1},{2,10},{10... | collective-permute-start | bytes 393224 | tf_op jit(solution)/shard_map/ppermute | solution.py:91
  9.0 1.4 %collective-permute-start.8 = (bf16[256,256]{1,0:T(8,128)(2,1)}, bf16[256,256]{1,0:T(8,128)(2,1)S(1)}, u32[]{:S(2)}, u32[]{:S(2)}) collective-permute-start(bf16[256,256]{1,0:T(8,128)(2,1)} %bitcast.21), channel_id=1, source_target_pairs={{0,24},{8,0},{16,8},{24,16},{1,25},{9,1},{17,9},{25,17},{2,26},{10... | collective-permute-start | bytes 393224 | tf_op jit(solution)/shard_map/ppermute | solution.py:91
  10.5 1.6 %collective-permute-start.9 = (bf16[256,256]{1,0:T(8,128)(2,1)}, bf16[256,256]{1,0:T(8,128)(2,1)S(1)}, u32[]{:S(2)}, u32[]{:S(2)}) collective-permute-start(bf16[256,256]{1,0:T(8,128)(2,1)} %bitcast.22), channel_id=1, source_target_pairs={{0,16},{8,24},{16,0},{24,8},{1,17},{9,25},{17,1},{25,9},{2,18},{10... | collective-permute-start | bytes 393224 | tf_op jit(solution)/shard_map/ppermute | solution.py:91
  12.1 2.5 %collective-permute-start.14 = (s32[1]{0:T(128)}, s32[1]{0:T(128)}, u32[]{:S(2)}, u32[]{:S(2)}) collective-permute-start(s32[1]{0:T(128)} %param.5), channel_id=1, source_target_pairs={{0,96},{32,0},{64,32},{96,64},{1,97},{33,1},{65,33},{97,65},{2,98}... | collective-permute-start | bytes 20 | tf_op jit(solution)/shard_map/ppermute | solution.py:92
  14.6 0.9 collective-permute-done.14
  15.4 2.3 %collective-permute-start.12 = (s32[1]{0:T(128)}, s32[1]{0:T(128)}, u32[]{:S(2)}, u32[]{:S(2)}) collective-permute-start(s32[1]{0:T(128)} %param.5), channel_id=1, source_target_pairs={{0,64},{32,96},{64,0},{96,32},{1,65},{33,97},{65,1},{97,33},{2,66}... | collective-permute-start | bytes 20 | tf_op jit(solution)/shard_map/ppermute | solution.py:92
  17.7 1.9 %collective-permute-done.12 = s32[1]{0:T(128)} collective-permute-done((s32[1]{0:T(128)}, s32[1]{0:T(128)}, u32[]{:S(2)}, u32[]{:S(2)}) %collective-permute-start.12) | collective-permute-done | bytes 36 | tf_op jit(solution)/shard_map/ppermute | solution.py:92
  19.6 0.7 collective-permute-start.4
  20.3 1.1 %collective-permute-start.5 = (bf16[256,256]{1,0:T(8,128)(2,1)S(1)}, bf16[256,256]{1,0:T(8,128)(2,1)S(1)}, u32[]{:S(2)}, u32[]{:S(2)}) collective-permute-start(bf16[256,256]{1,0:T(8,128)(2,1)S(1)} %collective-permute-done), channel_id=1, source_target_pairs={{0,24},{8,0},{16,8},{24,16},{1,25},{9,1},{17,9},{25,17},{2,26},{10... | collective-permute-start | bytes 393224 | tf_op jit(solution)/shard_map/ppermute | solution.py:93
  21.4 2.3 %collective-permute-done.4 = s32[1]{0:T(128)} collective-permute-done((s32[1]{0:T(128)}, s32[1]{0:T(128)}, u32[]{:S(2)}, u32[]{:S(2)}) %collective-permute-start.4) | collective-permute-done | bytes 36 | tf_op jit(solution)/shard_map/ppermute | solution.py:92
  23.7 1.3 %collective-permute-start.6 = (bf16[256,256]{1,0:T(8,128)(2,1)S(1)}, bf16[256,256]{1,0:T(8,128)(2,1)S(1)}, u32[]{:S(2)}, u32[]{:S(2)}) collective-permute-start(bf16[256,256]{1,0:T(8,128)(2,1)S(1)} %collective-permute-done), channel_id=1, source_target_pairs={{0,16},{8,24},{16,0},{24,8},{1,17},{9,25},{17,1},{25,9},{2,18},{10... | collective-permute-start | bytes 393224 | tf_op jit(solution)/shard_map/ppermute | solution.py:93
  25.0 0.2 collective-permute-start.7
  33.1 1.0 %select_select_fusion.1 = bf16[256,256]{1,0:T(8,128)(2,1)S(1)} fusion(bf16[256,256]{1,0:T(8,128)(2,1)S(1)} %collective-permute-done.5, bf16[256,256]{1,0:T(8,128)(2,1)S(1)} %collective-permute-done.6, bf16[256,256]{1,0:T(8,128)(2,1)S(1)} %collective-permute-done.7, bf16[256,256]{1,0:T(8,128)(2,1)S(1)} %collective-permute-done, ...), kind=kLoop, calls=%fused_computation.2 | loop fusion | flops 458752 | bytes 1179655 | tf_op jit(solution)/shard_map/jit(_where)/select_n | solution.py:79
  34.1 1.0 %select_select_fusion.2 = bf16[256,256]{1,0:T(8,128)(2,1)S(1)} fusion(bf16[256,256]{1,0:T(8,128)(2,1)S(1)} %collective-permute-done.5, bf16[256,256]{1,0:T(8,128)(2,1)S(1)} %collective-permute-done.6, bf16[256,256]{1,0:T(8,128)(2,1)S(1)} %collective-permute-done.7, bf16[256,256]{1,0:T(8,128)(2,1)S(1)} %collective-permute-done, ...), kind=kLoop, calls=%fused_computation.3 | loop fusion | flops 458752 | bytes 1179655 | tf_op jit(solution)/shard_map/jit(_where)/select_n | solution.py:79
  35.1 2.7 %collective-permute-start.13 = (bf16[256,256]{1,0:T(8,128)(2,1)S(1)}, bf16[256,256]{1,0:T(8,128)(2,1)S(1)}, u32[]{:S(2)}, u32[]{:S(2)}) collective-permute-start(bf16[256,256]{1,0:T(8,128)(2,1)S(1)} %select_select_fusion.2), channel_id=1, source_target_pairs={{0,64},{32,96},{64,0},{96,32},{1,65},{33,97},{65,1},{97,33},{2,66}... | collective-permute-start | bytes 393224 | tf_op jit(solution)/shard_map/ppermute | solution.py:99
  37.9 0.5 collective-permute-start.11
  38.4 0.7 constant_dynamic-slice_fusion
  39.1 0.7 collective-permute-start.19
  39.8 2.5 %collective-permute-start.20 = (bf16[24,2,256]{2,1,0:T(2,128)(2,1)S(1)}, bf16[24,2,256]{2,1,0:T(2,128)(2,1)S(1)}, u32[]{:S(2)}, u32[]{:S(2)}) collective-permute-start(bf16[24,2,256]{2,1,0:T(2,128)(2,1)S(1)} %get-tuple-element.10), channel_id=1, source_target_pairs={{0,6},{2,0},{4,2},{6,4},{1,7},{3,1},{5,3},{7,5},{8,14},{10,8},{12,... | collective-permute-start | bytes 73736 | tf_op jit(solution)/shard_map/ppermute | solution.py:107
  43.2 0.3 collective-permute-start.1
  43.5 3.2 %collective-permute-start.2 = (bf16[256,256]{1,0:T(8,128)(2,1)S(1)}, bf16[256,256]{1,0:T(8,128)(2,1)S(1)}, u32[]{:S(2)}, u32[]{:S(2)}) collective-permute-start(bf16[256,256]{1,0:T(8,128)(2,1)S(1)} %bitcast.26), channel_id=1, source_target_pairs={{0,6},{2,0},{4,2},{6,4},{1,7},{3,1},{5,3},{7,5},{8,14},{10,8},{12,... | collective-permute-start | bytes 393224 | tf_op jit(solution)/shard_map/ppermute | solution.py:103
  46.8 0.4 collective-permute-start.3
  47.3 3.2 %collective-permute-start.17 = (bf16[256,256]{1,0:T(8,128)(2,1)S(1)}, bf16[256,256]{1,0:T(8,128)(2,1)S(1)}, u32[]{:S(2)}, u32[]{:S(2)}) collective-permute-start(bf16[256,256]{1,0:T(8,128)(2,1)S(1)} %select_select_fusion.refs_4_), channel_id=1, source_target_pairs={{0,6},{2,0},{4,2},{6,4},{1,7},{3,1},{5,3},{7,5},{8,14},{10,8},{12,... | collective-permute-start | bytes 393224 | tf_op jit(solution)/shard_map/ppermute | solution.py:108
  50.5 0.3 collective-permute-start.18
  50.8 8.6 %collective-permute-done.3.refs_3_ = bf16[256,256]{1,0:T(8,128)(2,1)S(1)} collective-permute-done((bf16[256,256]{1,0:T(8,128)(2,1)S(1)}, bf16[256,256]{1,0:T(8,128)(2,1)S(1)}, u32[]{:S(2)}, u32[]{:S(2)}) %collective-permute-start.3) | collective-permute-done | bytes 131104 | tf_op jit(solution)/shard_map/ppermute | solution.py:103
  59.4 9.8 %collective-permute-done.18.refs_7_ = bf16[256,256]{1,0:T(8,128)(2,1)S(1)} collective-permute-done((bf16[256,256]{1,0:T(8,128)(2,1)S(1)}, bf16[256,256]{1,0:T(8,128)(2,1)S(1)}, u32[]{:S(2)}, u32[]{:S(2)}) %collective-permute-start.18) | collective-permute-done | bytes 131104 | tf_op jit(solution)/shard_map/ppermute | solution.py:108
  69.2 0.6 copy-done.7
  69.8 5.9 %shard_map.38 = f32[12,2,128,128]{3,2,1,0:T(8,128)} custom-call(s32[1]{0:T(128)} %bitcast.6.half_ref, bf16[256,256]{1,0:T(8,128)(2,1)} %bitcast.23, bf16[256,256]{1,0:T(8,128)(2,1)} %copy-done.2, bf16[256,256]{1,0:T(8,128)(2,1)} %copy-done.3, bf16[256,256]{1,0:T(8,128)(2,1)} %copy-done.4, bf16[256,256]{1,0:T(8,128)(2,1)} %copy-done.1, ...), custom_call_target="tpu_custom_call" | custom-call | tf_op jit(solution)/shard_map/pallas_call | solution.py:59
  75.7 2.7 %collective-permute-start.22 = (f32[12,2,128,128]{3,2,1,0:T(8,128)}, f32[12,2,128,128]{3,2,1,0:T(8,128)S(1)}, u32[]{:S(2)}, u32[]{:S(2)}) collective-permute-start(f32[12,2,128,128]{3,2,1,0:T(8,128)} %shard_map.38), channel_id=1, source_target_pairs={{0,1},{1,0},{2,3},{3,2},{4,5},{5,4},{6,7},{7,6},{8,9},{9,8},{10,11... | collective-permute-start | bytes 4718600 | tf_op jit(solution)/shard_map/ppermute | solution.py:111
  78.4 5.8 %shard_map.37 = f32[12,2,128,128]{3,2,1,0:T(8,128)} custom-call(s32[1]{0:T(128)} %bitcast.half_ref, bf16[256,256]{1,0:T(8,128)(2,1)} %bitcast.24, bf16[256,256]{1,0:T(8,128)(2,1)} %copy-done.2, bf16[256,256]{1,0:T(8,128)(2,1)} %copy-done.3, bf16[256,256]{1,0:T(8,128)(2,1)} %copy-done.4, bf16[256,256]{1,0:T(8,128)(2,1)} %copy-done.1, ...), custom_call_target="tpu_custom_call" | custom-call | tf_op jit(solution)/shard_map/pallas_call | solution.py:59
  84.2 2.7 %add_bitcast_fusion = f32[12,1,2,128,128]{4,3,2,1,0:T(8,128)} fusion(f32[12,2,128,128]{3,2,1,0:T(8,128)} %shard_map.37, f32[12,2,128,128]{3,2,1,0:T(8,128)S(1)} %collective-permute-done.22), kind=kLoop, calls=%fused_computation | loop fusion | flops 393216 | bytes 4718592 | tf_op jit(solution)/shard_map/broadcast_in_dim | solution.py:113
  (46 shorter events, 0.5 us)
Async XLA Ops:
  0.0 37.8 %copy-start = (bf16[1,2,128,256]{3,2,1,0:T(8,128)(2,1)S(1)}, bf16[1,2,128,256]{3,2,1,0:T(8,128)(2,1)}, u32[]{:S(2)}) copy-start(bf16[1,2,128,256]{3,2,1,0:T(8,128)(2,1)} %param.3) | copy-start | bytes 393220
  0.0 20.3 %collective-permute-start = (bf16[256,256]{1,0:T(8,128)(2,1)}, bf16[256,256]{1,0:T(8,128)(2,1)S(1)}, u32[]{:S(2)}, u32[]{:S(2)}) collective-permute-start(bf16[256,256]{1,0:T(8,128)(2,1)} %bitcast.19), channel_id=1, source_target_pairs={{0,128},{128,0},{1,129},{129,1},{2,130},{130,2},{3,131},{131,3},{4... | collective-permute-start | bytes 393224 | tf_op jit(solution)/shard_map/ppermute | solution.py:90
  7.7 17.3 %collective-permute-start.10 = (bf16[256,256]{1,0:T(8,128)(2,1)}, bf16[256,256]{1,0:T(8,128)(2,1)S(1)}, u32[]{:S(2)}, u32[]{:S(2)}) collective-permute-start(bf16[256,256]{1,0:T(8,128)(2,1)} %bitcast.20), channel_id=1, source_target_pairs={{0,8},{8,16},{16,24},{24,0},{1,9},{9,17},{17,25},{25,1},{2,10},{10... | collective-permute-start | bytes 393224 | tf_op jit(solution)/shard_map/ppermute | solution.py:91
  9.0 24.0 %collective-permute-start.8 = (bf16[256,256]{1,0:T(8,128)(2,1)}, bf16[256,256]{1,0:T(8,128)(2,1)S(1)}, u32[]{:S(2)}, u32[]{:S(2)}) collective-permute-start(bf16[256,256]{1,0:T(8,128)(2,1)} %bitcast.21), channel_id=1, source_target_pairs={{0,24},{8,0},{16,8},{24,16},{1,25},{9,1},{17,9},{25,17},{2,26},{10... | collective-permute-start | bytes 393224 | tf_op jit(solution)/shard_map/ppermute | solution.py:91
  10.5 22.6 %collective-permute-start.9 = (bf16[256,256]{1,0:T(8,128)(2,1)}, bf16[256,256]{1,0:T(8,128)(2,1)S(1)}, u32[]{:S(2)}, u32[]{:S(2)}) collective-permute-start(bf16[256,256]{1,0:T(8,128)(2,1)} %bitcast.22), channel_id=1, source_target_pairs={{0,16},{8,24},{16,0},{24,8},{1,17},{9,25},{17,1},{25,9},{2,18},{10... | collective-permute-start | bytes 393224 | tf_op jit(solution)/shard_map/ppermute | solution.py:91
  12.1 3.3 %collective-permute-start.14 = (s32[1]{0:T(128)}, s32[1]{0:T(128)}, u32[]{:S(2)}, u32[]{:S(2)}) collective-permute-start(s32[1]{0:T(128)} %param.5), channel_id=1, source_target_pairs={{0,96},{32,0},{64,32},{96,64},{1,97},{33,1},{65,33},{97,65},{2,98}... | collective-permute-start | bytes 20 | tf_op jit(solution)/shard_map/ppermute | solution.py:92
  15.4 4.2 %collective-permute-start.12 = (s32[1]{0:T(128)}, s32[1]{0:T(128)}, u32[]{:S(2)}, u32[]{:S(2)}) collective-permute-start(s32[1]{0:T(128)} %param.5), channel_id=1, source_target_pairs={{0,64},{32,96},{64,0},{96,32},{1,65},{33,97},{65,1},{97,33},{2,66}... | collective-permute-start | bytes 20 | tf_op jit(solution)/shard_map/ppermute | solution.py:92
  19.6 4.1 %collective-permute-start.4 = (s32[1]{0:T(128)}, s32[1]{0:T(128)}, u32[]{:S(2)}, u32[]{:S(2)}) collective-permute-start(s32[1]{0:T(128)} %param.5), channel_id=1, source_target_pairs={{0,32},{32,64},{64,96},{96,0},{1,33},{33,65},{65,97},{97,1},{2,34}... | collective-permute-start | bytes 20 | tf_op jit(solution)/shard_map/ppermute | solution.py:92
  20.3 12.7 %collective-permute-start.5 = (bf16[256,256]{1,0:T(8,128)(2,1)S(1)}, bf16[256,256]{1,0:T(8,128)(2,1)S(1)}, u32[]{:S(2)}, u32[]{:S(2)}) collective-permute-start(bf16[256,256]{1,0:T(8,128)(2,1)S(1)} %collective-permute-done), channel_id=1, source_target_pairs={{0,24},{8,0},{16,8},{24,16},{1,25},{9,1},{17,9},{25,17},{2,26},{10... | collective-permute-start | bytes 393224 | tf_op jit(solution)/shard_map/ppermute | solution.py:93
  23.7 9.4 %collective-permute-start.6 = (bf16[256,256]{1,0:T(8,128)(2,1)S(1)}, bf16[256,256]{1,0:T(8,128)(2,1)S(1)}, u32[]{:S(2)}, u32[]{:S(2)}) collective-permute-start(bf16[256,256]{1,0:T(8,128)(2,1)S(1)} %collective-permute-done), channel_id=1, source_target_pairs={{0,16},{8,24},{16,0},{24,8},{1,17},{9,25},{17,1},{25,9},{2,18},{10... | collective-permute-start | bytes 393224 | tf_op jit(solution)/shard_map/ppermute | solution.py:93
  25.0 8.1 %collective-permute-start.7 = (bf16[256,256]{1,0:T(8,128)(2,1)S(1)}, bf16[256,256]{1,0:T(8,128)(2,1)S(1)}, u32[]{:S(2)}, u32[]{:S(2)}) collective-permute-start(bf16[256,256]{1,0:T(8,128)(2,1)S(1)} %collective-permute-done), channel_id=1, source_target_pairs={{0,8},{8,16},{16,24},{24,0},{1,9},{9,17},{17,25},{25,1},{2,10},{10... | collective-permute-start | bytes 393224 | tf_op jit(solution)/shard_map/ppermute | solution.py:93
  34.1 9.0 %collective-permute-start.15 = (bf16[256,256]{1,0:T(8,128)(2,1)S(1)}, bf16[256,256]{1,0:T(8,128)(2,1)S(1)}, u32[]{:S(2)}, u32[]{:S(2)}) collective-permute-start(bf16[256,256]{1,0:T(8,128)(2,1)S(1)} %select_select_fusion.1), channel_id=1, source_target_pairs={{0,32},{32,64},{64,96},{96,0},{1,33},{33,65},{65,97},{97,1},{2,34}... | collective-permute-start | bytes 393224 | tf_op jit(solution)/shard_map/ppermute | solution.py:99
  35.1 8.1 %collective-permute-start.13 = (bf16[256,256]{1,0:T(8,128)(2,1)S(1)}, bf16[256,256]{1,0:T(8,128)(2,1)S(1)}, u32[]{:S(2)}, u32[]{:S(2)}) collective-permute-start(bf16[256,256]{1,0:T(8,128)(2,1)S(1)} %select_select_fusion.2), channel_id=1, source_target_pairs={{0,64},{32,96},{64,0},{96,32},{1,65},{33,97},{65,1},{97,33},{2,66}... | collective-permute-start | bytes 393224 | tf_op jit(solution)/shard_map/ppermute | solution.py:99
  37.9 5.6 %collective-permute-start.11 = (bf16[256,256]{1,0:T(8,128)(2,1)S(1)}, bf16[256,256]{1,0:T(8,128)(2,1)S(1)}, u32[]{:S(2)}, u32[]{:S(2)}) collective-permute-start(bf16[256,256]{1,0:T(8,128)(2,1)S(1)} %select_select_fusion.3), channel_id=1, source_target_pairs={{0,96},{32,0},{64,32},{96,64},{1,97},{33,1},{65,33},{97,65},{2,98}... | collective-permute-start | bytes 393224 | tf_op jit(solution)/shard_map/ppermute | solution.py:99
  39.1 7.8 %collective-permute-start.19 = (bf16[24,2,256]{2,1,0:T(2,128)(2,1)S(1)}, bf16[24,2,256]{2,1,0:T(2,128)(2,1)S(1)}, u32[]{:S(2)}, u32[]{:S(2)}) collective-permute-start(bf16[24,2,256]{2,1,0:T(2,128)(2,1)S(1)} %get-tuple-element.8), channel_id=1, source_target_pairs={{0,2},{2,4},{4,6},{6,0},{1,3},{3,5},{5,7},{7,1},{8,10},{10,12},{12... | collective-permute-start | bytes 73736 | tf_op jit(solution)/shard_map/ppermute | solution.py:107
  39.8 7.4 %collective-permute-start.20 = (bf16[24,2,256]{2,1,0:T(2,128)(2,1)S(1)}, bf16[24,2,256]{2,1,0:T(2,128)(2,1)S(1)}, u32[]{:S(2)}, u32[]{:S(2)}) collective-permute-start(bf16[24,2,256]{2,1,0:T(2,128)(2,1)S(1)} %get-tuple-element.10), channel_id=1, source_target_pairs={{0,6},{2,0},{4,2},{6,4},{1,7},{3,1},{5,3},{7,5},{8,14},{10,8},{12,... | collective-permute-start | bytes 73736 | tf_op jit(solution)/shard_map/ppermute | solution.py:107
  43.1 4.2 %collective-permute-start.21 = (bf16[24,2,256]{2,1,0:T(2,128)(2,1)S(1)}, bf16[24,2,256]{2,1,0:T(2,128)(2,1)S(1)}, u32[]{:S(2)}, u32[]{:S(2)}) collective-permute-start(bf16[24,2,256]{2,1,0:T(2,128)(2,1)S(1)} %get-tuple-element.7), channel_id=1, source_target_pairs={{0,4},{2,6},{4,0},{6,2},{1,5},{3,7},{5,1},{7,3},{8,12},{10,14},{12... | collective-permute-start | bytes 73736 | tf_op jit(solution)/shard_map/ppermute | solution.py:107
  43.2 7.3 %collective-permute-start.1 = (bf16[256,256]{1,0:T(8,128)(2,1)S(1)}, bf16[256,256]{1,0:T(8,128)(2,1)S(1)}, u32[]{:S(2)}, u32[]{:S(2)}) collective-permute-start(bf16[256,256]{1,0:T(8,128)(2,1)S(1)} %bitcast.25), channel_id=1, source_target_pairs={{0,2},{2,4},{4,6},{6,0},{1,3},{3,5},{5,7},{7,1},{8,10},{10,12},{12... | collective-permute-start | bytes 393224 | tf_op jit(solution)/shard_map/ppermute | solution.py:103
  43.5 7.3 %collective-permute-start.2 = (bf16[256,256]{1,0:T(8,128)(2,1)S(1)}, bf16[256,256]{1,0:T(8,128)(2,1)S(1)}, u32[]{:S(2)}, u32[]{:S(2)}) collective-permute-start(bf16[256,256]{1,0:T(8,128)(2,1)S(1)} %bitcast.26), channel_id=1, source_target_pairs={{0,6},{2,0},{4,2},{6,4},{1,7},{3,1},{5,3},{7,5},{8,14},{10,8},{12,... | collective-permute-start | bytes 393224 | tf_op jit(solution)/shard_map/ppermute | solution.py:103
  46.8 22.4 %copy-start.1 = (bf16[256,256]{1,0:T(8,128)(2,1)}, bf16[256,256]{1,0:T(8,128)(2,1)S(1)}, u32[]{:S(2)}) copy-start(bf16[256,256]{1,0:T(8,128)(2,1)S(1)} %select_select_fusion.refs_4_) | copy-start | bytes 393220
  46.8 22.3 %copy-start.8 = (bf16[24,2,256]{2,1,0:T(2,128)(2,1)}, bf16[24,2,256]{2,1,0:T(2,128)(2,1)S(1)}, u32[]{:S(2)}) copy-start(bf16[24,2,256]{2,1,0:T(2,128)(2,1)S(1)} %collective-permute-done.19.refs_9_) | copy-start | bytes 73732
  46.8 12.5 %collective-permute-start.3 = (bf16[256,256]{1,0:T(8,128)(2,1)S(1)}, bf16[256,256]{1,0:T(8,128)(2,1)S(1)}, u32[]{:S(2)}, u32[]{:S(2)}) collective-permute-start(bf16[256,256]{1,0:T(8,128)(2,1)S(1)} %bitcast.27), channel_id=1, source_target_pairs={{0,4},{2,6},{4,0},{6,2},{1,5},{3,7},{5,1},{7,3},{8,12},{10,14},{12... | collective-permute-start | bytes 393224 | tf_op jit(solution)/shard_map/ppermute | solution.py:103
  47.2 22.0 %copy-start.9 = (bf16[24,2,256]{2,1,0:T(2,128)(2,1)}, bf16[24,2,256]{2,1,0:T(2,128)(2,1)S(1)}, u32[]{:S(2)}) copy-start(bf16[24,2,256]{2,1,0:T(2,128)(2,1)S(1)} %collective-permute-done.20.refs_10_) | copy-start | bytes 73732
  47.2 12.1 %collective-permute-start.16 = (bf16[256,256]{1,0:T(8,128)(2,1)S(1)}, bf16[256,256]{1,0:T(8,128)(2,1)S(1)}, u32[]{:S(2)}, u32[]{:S(2)}) collective-permute-start(bf16[256,256]{1,0:T(8,128)(2,1)S(1)} %select_select_fusion.refs_4_), channel_id=1, source_target_pairs={{0,2},{2,4},{4,6},{6,0},{1,3},{3,5},{5,7},{7,1},{8,10},{10,12},{12... | collective-permute-start | bytes 393224 | tf_op jit(solution)/shard_map/ppermute | solution.py:108
  47.3 21.9 %copy-start.10 = (bf16[24,2,256]{2,1,0:T(2,128)(2,1)}, bf16[24,2,256]{2,1,0:T(2,128)(2,1)S(1)}, u32[]{:S(2)}) copy-start(bf16[24,2,256]{2,1,0:T(2,128)(2,1)S(1)} %collective-permute-done.21.refs_11_) | copy-start | bytes 73732
  47.3 12.0 %collective-permute-start.17 = (bf16[256,256]{1,0:T(8,128)(2,1)S(1)}, bf16[256,256]{1,0:T(8,128)(2,1)S(1)}, u32[]{:S(2)}, u32[]{:S(2)}) collective-permute-start(bf16[256,256]{1,0:T(8,128)(2,1)S(1)} %select_select_fusion.refs_4_), channel_id=1, source_target_pairs={{0,6},{2,0},{4,2},{6,4},{1,7},{3,1},{5,3},{7,5},{8,14},{10,8},{12,... | collective-permute-start | bytes 393224 | tf_op jit(solution)/shard_map/ppermute | solution.py:108
  50.5 18.7 %copy-start.2 = (bf16[256,256]{1,0:T(8,128)(2,1)}, bf16[256,256]{1,0:T(8,128)(2,1)S(1)}, u32[]{:S(2)}) copy-start(bf16[256,256]{1,0:T(8,128)(2,1)S(1)} %collective-permute-done.1.refs_1_) | copy-start | bytes 393220
  50.5 18.7 %collective-permute-start.18 = (bf16[256,256]{1,0:T(8,128)(2,1)S(1)}, bf16[256,256]{1,0:T(8,128)(2,1)S(1)}, u32[]{:S(2)}, u32[]{:S(2)}) collective-permute-start(bf16[256,256]{1,0:T(8,128)(2,1)S(1)} %select_select_fusion.refs_4_), channel_id=1, source_target_pairs={{0,4},{2,6},{4,0},{6,2},{1,5},{3,7},{5,1},{7,3},{8,12},{10,14},{12... | collective-permute-start | bytes 393224 | tf_op jit(solution)/shard_map/ppermute | solution.py:108
  50.8 18.4 %copy-start.3 = (bf16[256,256]{1,0:T(8,128)(2,1)}, bf16[256,256]{1,0:T(8,128)(2,1)S(1)}, u32[]{:S(2)}) copy-start(bf16[256,256]{1,0:T(8,128)(2,1)S(1)} %collective-permute-done.2.refs_2_) | copy-start | bytes 393220
  59.3 9.9 %copy-start.5 = (bf16[256,256]{1,0:T(8,128)(2,1)}, bf16[256,256]{1,0:T(8,128)(2,1)S(1)}, u32[]{:S(2)}) copy-start(bf16[256,256]{1,0:T(8,128)(2,1)S(1)} %collective-permute-done.16.refs_5_) | copy-start | bytes 393220
  59.4 9.9 %copy-start.6 = (bf16[256,256]{1,0:T(8,128)(2,1)}, bf16[256,256]{1,0:T(8,128)(2,1)S(1)}, u32[]{:S(2)}) copy-start(bf16[256,256]{1,0:T(8,128)(2,1)S(1)} %collective-permute-done.17.refs_6_) | copy-start | bytes 393220
  75.7 8.6 %collective-permute-start.22 = (f32[12,2,128,128]{3,2,1,0:T(8,128)}, f32[12,2,128,128]{3,2,1,0:T(8,128)S(1)}, u32[]{:S(2)}, u32[]{:S(2)}) collective-permute-start(f32[12,2,128,128]{3,2,1,0:T(8,128)} %shard_map.38), channel_id=1, source_target_pairs={{0,1},{1,0},{2,3},{3,2},{4,5},{5,4},{6,7},{7,6},{8,9},{9,8},{10,11... | collective-permute-start | bytes 4718600 | tf_op jit(solution)/shard_map/ppermute | solution.py:111
  (3 other events, 15.9 us)

commit v2 on v1

v2 whole, which is shorter than its diff:
```python
import jax
import jax.numpy as jnp
from jax import lax
from jax.experimental import pallas as pl
from jax.experimental.pallas import tpu as pltpu
from jax.sharding import Mesh
from jax.sharding import PartitionSpec as P

KA = ("zh", "x", "y")
GA = ("zl", "c")
SWAP = [(0, 1), (1, 0)]
STEPS = (1, 3, 2)


def ring(step, size=4):
    return [(i, (i + step) % size) for i in range(size)]


def pack(zl, slab, potential):
    rows, cells = slab.shape
    share = potential.shape[0] // 4

    def kernel(zl_ref, slab_ref, pot_ref, *outs):
        for s, out in enumerate(outs):
            out[:rows] = slab_ref[...]
            first = pl.multiple_of(share * lax.rem(zl_ref[0] + s, 4), share)
            out[rows:] = pot_ref[pl.ds(first, share), :]

    return pl.pallas_call(
        kernel,
        in_specs=[pl.BlockSpec(memory_space=pltpu.SMEM), pl.BlockSpec(memory_space=pltpu.VMEM), pl.BlockSpec(memory_space=pltpu.VMEM)],
        out_shape=[jax.ShapeDtypeStruct((rows + share, cells), slab.dtype)] * 4,
    )(zl, slab, potential)


def couple(core, packs, others, bands, modes, per_step):
    parts = len(others)
    cells = others[0].shape[1]
    wide = parts * cells
    rows = 2 * bands
    share = packs[0].shape[-2] - rows
    count = len(packs)

    def kernel(core_ref, *refs):
        pack_refs, other_refs = refs[:count], refs[count : count + parts]
        out_ref = refs[count + parts]
        wave_re, wave_im, pots, left, right_a, right_b = refs[count + parts + 1 :]
        step = pl.program_id(0)
        first = core_ref[0] * (share // 2)
        pieces = []
        for ref in pack_refs:
            if len(ref.shape) == 3:
                pieces += [ref.at[i] for i in range(ref.shape[0])]
            else:
                pieces.append(ref)

        def fill(mode, right):
            for p in range(parts):
                at = slice(p * cells, (p + 1) * cells)
                dv_re = pots[pl.ds(first + 2 * mode, 1), at]
                dv_im = pots[pl.ds(first + 2 * mode + 1, 1), at]
                w_re, w_im = wave_re[:, at], wave_im[:, at]
                right[:bands, at] = (dv_re * w_re - dv_im * w_im).astype(jnp.bfloat16)
                right[bands:, at] = (dv_re * w_im + dv_im * w_re).astype(jnp.bfloat16)

        def finish(slot, right):
            full = lax.dot_general(left[...], right[...], (((1,), (1,)), ((), ())), preferred_element_type=jnp.float32)
            out_ref[slot, 0] = full[:bands, :bands] + full[bands:, bands:]
            out_ref[slot, 1] = full[:bands, bands:] - full[bands:, :bands]

        @pl.when(step == 0)
        def _():
            for p in range(parts):
                at = slice(p * cells, (p + 1) * cells)
                wave_re[:, at] = pieces[p][:bands].astype(jnp.float32)
                wave_im[:, at] = pieces[p][bands:rows].astype(jnp.float32)
                pots[:, at] = pieces[p][rows:].astype(jnp.float32)
                left[:, at] = other_refs[p][...]

        for j in range(0, per_step, 2):
            fill(step * per_step + j, right_a)
            fill(step * per_step + j + 1, right_b)
            finish(j, right_a)
            finish(j + 1, right_b)

    whole = lambda a: pl.BlockSpec(a.shape, lambda i: (0,) * a.ndim)
    return pl.pallas_call(
        kernel,
        grid=(modes // per_step,),
        in_specs=[pl.BlockSpec(memory_space=pltpu.SMEM)] + [whole(a) for a in (*packs, *others)],
        out_specs=pl.BlockSpec((per_step, 2, bands, bands), lambda i: (i, 0, 0, 0)),
        out_shape=jax.ShapeDtypeStruct((modes, 2, bands, bands), jnp.float32),
        scratch_shapes=[
            pltpu.VMEM((bands, wide), jnp.float32),
            pltpu.VMEM((bands, wide), jnp.float32),
            pltpu.VMEM((share, wide), jnp.float32),
            pltpu.VMEM((rows, wide), jnp.bfloat16),
            pltpu.VMEM((rows, wide), jnp.bfloat16),
            pltpu.VMEM((rows, wide), jnp.bfloat16),
        ],
        compiler_params=pltpu.CompilerParams(dimension_semantics=("arbitrary",)),
    )(core, *packs, *others)


def pick(number, choices):
    out = choices[0]
    for i, choice in enumerate(choices[1:], 1):
        out = jnp.where(number == i, choice, out)
    return out


def body(psi, dvscf, kq_map):
    zh, x, y, zl, c = (lax.axis_index(a) for a in ("zh", "x", "y", "zl", "c"))
    bands, cells = psi.shape[2], psi.shape[3]
    modes = dvscf.shape[0] // 8
    slab = psi.reshape(2 * bands, cells)

    swapped = lax.ppermute(slab, "zh", SWAP)
    near = [slab] + [lax.ppermute(slab, "y", ring(s)) for s in (1, 2, 3)]
    far = [swapped] + [lax.ppermute(swapped, "y", ring(s)) for s in (1, 2, 3)]
    wanted = [kq_map] + [lax.ppermute(kq_map, "x", ring(-s)) for s in (1, 2, 3)]

    packs = pack(zl[None], slab, dvscf.reshape(-1, cells))
    lines = [packs[0]] + [lax.ppermute(packs[s], "zl", ring(s)) for s in STEPS]
    lines = jnp.stack(lines)
    twins = lax.ppermute(lines, "c", SWAP)

    slots = []
    for k in wanted:
        source = k[0]
        back = (y - source % 4) % 4
        slots.append(pick(jnp.where(source // 16 == zh, back, back + 4), near + far))
    came = [slots[0]] + [lax.ppermute(slots[s], "x", ring(s)) for s in (1, 2, 3)]
    phi = pick((x - (kq_map[0] // 4) % 4) % 4, came)

    others = [phi] + [lax.ppermute(phi, "zl", ring(s)) for s in STEPS]
    others += [lax.ppermute(o, "c", SWAP) for o in others]
    out = couple(c[None], [lines, twins], others, bands, modes, 4)
    return out[:, None]


def solution(mesh):
    finer = Mesh(mesh.devices.reshape(2, 4, 4, 4, 2), KA + GA)
    in_specs = (P(KA, None, None, GA), P(None, None, GA), P(KA))
    out_specs = P(GA, KA, None, None, None)
    return jax.shard_map(body, mesh=finer, in_specs=in_specs, out_specs=out_specs, check_vma=False)
```

time: 87.3 us -> 74.8 us (0.86)
  waiting for transfers between devices: 23.4 us -> 11 us
  starting transfers between devices: 37 us -> 42.7 us
  other arithmetic: 4.78 us -> 1.28 us
  Pallas kernels: 11.7 us -> 8.56 us
  local copies, waits for them, and re-layouts: 1.29 us -> 2.46 us
    ppermute x10 -> x11, waiting for transfers between devices: 18.4 us -> 8.55 us  [the longest x3 7.52 us: body(): lines = [packs[0]] + [lax.ppermute(packs[s], 'zl', ring(s)) for s in STEPS]]
    ppermute x10 -> x11, starting transfers between devices: 13.5 us -> 20 us  [the longest x4 11.5 us: body(): others += [lax.ppermute(o, 'c', SWAP) for o in others]]
    pallas_call x2, Pallas kernels: 11.7 us -> 8.56 us  [the longest x1 6.75 us: couple(): pl.pallas_call(kernel, grid=(modes // per_step,), in_specs=[pl.BlockSpec(...]
    broadcast_in_dim x1 -> x0, other arithmetic: 2.72 us -> none  [body(): return (mine + theirs)[:, None]]
    ppermute x3, waiting for transfers between devices: 5.04 us -> 2.42 us  [body(): wanted = [kq_map] + [lax.ppermute(kq_map, 'x', ring(-s)) for s in (1, 2, 3)]]
    reshape x0 -> x1, local copies, waits for them, and re-layouts: none -> 1.57 us  [body(): packs = pack(zl[None], slab, dvscf.reshape(-1, cells))]
    ppermute x3, starting transfers between devices: 5.46 us -> 4.21 us  [body(): wanted = [kq_map] + [lax.ppermute(kq_map, 'x', ring(-s)) for s in (1, 2, 3)]]
  transfers between devices with their start and end apart: 23 -> 24, of which waited for: 5 -> 5; matrix products, arithmetic and copies ran while one was open for 2% -> 4% of each run, Pallas kernels for 7% -> 2%
where the time goes in v2:
time: 74.8 us; the launch traced here: 74.5 us
  starting transfers between devices  42.7 us (57%)
  waiting for transfers between devices  11 us (15%)
  Pallas kernels  8.56 us (11%)
  between operations  8.56 us (11%)
  local copies, waits for them, and re-layouts  2.46 us (3%)
  other arithmetic  1.28 us (2%)
    ppermute x4, starting transfers between devices, body(): others += [lax.ppermute(o, 'c', SWAP) for o in others]  11.5 us
    ppermute x1, starting transfers between devices, body(): swapped = lax.ppermute(slab, 'zh', SWAP)  7.73 us
    ppermute x3, waiting for transfers between devices, body(): lines = [packs[0]] + [lax.ppermute(packs[s], 'zl', ring(s)) for s in STEPS]  7.52 us
    pallas_call x1, Pallas kernels, couple(): pl.pallas_call(kernel, grid=(modes // per_step,), in_specs=[pl.BlockSpec(...  6.75 us
    ppermute x3, starting transfers between devices, body(): near = [slab] + [lax.ppermute(slab, 'y', ring(s)) for s in (1, 2, 3)]  4.99 us
    ppermute x3, starting transfers between devices, body(): wanted = [kq_map] + [lax.ppermute(kq_map, 'x', ring(-s)) for s in (1, 2, 3)]  4.21 us
    ppermute x1, starting transfers between devices, body(): twins = lax.ppermute(lines, 'c', SWAP)  3.37 us
    ppermute x3, starting transfers between devices, body(): lines = [packs[0]] + [lax.ppermute(packs[s], 'zl', ring(s)) for s in STEPS]  3.34 us
  transfers between devices with their start and end apart: 24, of which 5 were waited for; matrix products, arithmetic and copies ran while one was open for 4% of the time, Pallas kernels for 2%

profile of v2, /device:TPU:1, one launch (start us, length us, event | category | flops | bytes accessed | tf_op | source)
XLA Modules:
  0.0 74.5 jit_solution(15106860591319277605)
XLA Ops:
  0.0 7.7 %collective-permute-start.5 = (bf16[256,256]{1,0:T(8,128)(2,1)}, bf16[256,256]{1,0:T(8,128)(2,1)S(1)}, u32[]{:S(2)}, u32[]{:S(2)}) collective-permute-start(bf16[256,256]{1,0:T(8,128)(2,1)} %bitcast.22), channel_id=1, source_target_pairs={{0,128},{128,0},{1,129},{129,1},{2,130},{130,2},{3,131},{131,3},{4... | collective-permute-start | bytes 393224 | tf_op jit(solution)/shard_map/ppermute | solution.py:118
  7.7 1.3 %collective-permute-start.11 = (bf16[256,256]{1,0:T(8,128)(2,1)}, bf16[256,256]{1,0:T(8,128)(2,1)S(1)}, u32[]{:S(2)}, u32[]{:S(2)}) collective-permute-start(bf16[256,256]{1,0:T(8,128)(2,1)} %bitcast.23), channel_id=1, source_target_pairs={{0,8},{8,16},{16,24},{24,0},{1,9},{9,17},{17,25},{25,1},{2,10},{10... | collective-permute-start | bytes 393224 | tf_op jit(solution)/shard_map/ppermute | solution.py:119
  9.0 1.2 %collective-permute-start.4 = (s32[1]{0:T(128)}, s32[1]{0:T(128)}, u32[]{:S(2)}, u32[]{:S(2)}) collective-permute-start(s32[1]{0:T(128)} %param.5), channel_id=1, source_target_pairs={{0,32},{32,64},{64,96},{96,0},{1,33},{33,65},{65,97},{97,1},{2,34}... | collective-permute-start | bytes 20 | tf_op jit(solution)/shard_map/ppermute | solution.py:121
  10.2 1.5 %collective-permute-start.15 = (s32[1]{0:T(128)}, s32[1]{0:T(128)}, u32[]{:S(2)}, u32[]{:S(2)}) collective-permute-start(s32[1]{0:T(128)} %param.5), channel_id=1, source_target_pairs={{0,96},{32,0},{64,32},{96,64},{1,97},{33,1},{65,33},{97,65},{2,98}... | collective-permute-start | bytes 20 | tf_op jit(solution)/shard_map/ppermute | solution.py:121
  11.7 2.6 %collective-permute-start.10 = (bf16[256,256]{1,0:T(8,128)(2,1)}, bf16[256,256]{1,0:T(8,128)(2,1)S(1)}, u32[]{:S(2)}, u32[]{:S(2)}) collective-permute-start(bf16[256,256]{1,0:T(8,128)(2,1)} %bitcast.24), channel_id=1, source_target_pairs={{0,16},{8,24},{16,0},{24,8},{1,17},{9,25},{17,1},{25,9},{2,18},{10... | collective-permute-start | bytes 393224 | tf_op jit(solution)/shard_map/ppermute | solution.py:119
  14.3 1.1 %collective-permute-start.9 = (bf16[256,256]{1,0:T(8,128)(2,1)}, bf16[256,256]{1,0:T(8,128)(2,1)S(1)}, u32[]{:S(2)}, u32[]{:S(2)}) collective-permute-start(bf16[256,256]{1,0:T(8,128)(2,1)} %bitcast.25), channel_id=1, source_target_pairs={{0,24},{8,0},{16,8},{24,16},{1,25},{9,1},{17,9},{25,17},{2,26},{10... | collective-permute-start | bytes 393224 | tf_op jit(solution)/shard_map/ppermute | solution.py:119
  15.4 1.5 %collective-permute-start.13 = (s32[1]{0:T(128)}, s32[1]{0:T(128)}, u32[]{:S(2)}, u32[]{:S(2)}) collective-permute-start(s32[1]{0:T(128)} %param.5), channel_id=1, source_target_pairs={{0,64},{32,96},{64,0},{96,32},{1,65},{33,97},{65,1},{97,33},{2,66}... | collective-permute-start | bytes 20 | tf_op jit(solution)/shard_map/ppermute | solution.py:121
  16.9 0.4 collective-permute-start.8
  17.3 2.4 %collective-permute-done.13 = s32[1]{0:T(128)} collective-permute-done((s32[1]{0:T(128)}, s32[1]{0:T(128)}, u32[]{:S(2)}, u32[]{:S(2)}) %collective-permute-start.13) | collective-permute-done | bytes 36 | tf_op jit(solution)/shard_map/ppermute | solution.py:121
  19.8 0.2 collective-permute-start.7
  20.0 2.4 %collective-permute-start.6 = (bf16[256,256]{1,0:T(8,128)(2,1)S(1)}, bf16[256,256]{1,0:T(8,128)(2,1)S(1)}, u32[]{:S(2)}, u32[]{:S(2)}) collective-permute-start(bf16[256,256]{1,0:T(8,128)(2,1)S(1)} %collective-permute-done.5), channel_id=1, source_target_pairs={{0,24},{8,0},{16,8},{24,16},{1,25},{9,1},{17,9},{25,17},{2,26},{10... | collective-permute-start | bytes 393224 | tf_op jit(solution)/shard_map/ppermute | solution.py:120
  22.4 1.6 %reshape.7.pot_ref = bf16[192,256]{1,0:T(8,128)(2,1)} reshape(bf16[96,2,256]{2,1,0:T(2,128)(2,1)} %param.4) | data formatting | bytes 196608 | tf_op jit(solution)/shard_map/reshape | solution.py:123
  23.9 1.8 %shard_map.37 = (bf16[304,256]{1,0:T(8,128)(2,1)}, bf16[304,256]{1,0:T(8,128)(2,1)}, bf16[304,256]{1,0:T(8,128)(2,1)}, bf16[304,256]{1,0:T(8,128)(2,1)}) custom-call(s32[1]{0:T(128)} %bitcast.1.zl_ref, bf16[256,256]{1,0:T(8,128)(2,1)} %bitcast.26, bf16[192,256]{1,0:T(8,128)(2,1)} %reshape.7.pot_ref), custom_call_target="tpu_custom_call" | custom-call | tf_op jit(solution)/shard_map/pallas_call | solution.py:29
  33.4 0.8 %collective-permute-start = (bf16[304,256]{1,0:T(8,128)(2,1)}, bf16[304,256]{1,0:T(8,128)(2,1)S(1)}, u32[]{:S(2)}, u32[]{:S(2)}) collective-permute-start(bf16[304,256]{1,0:T(8,128)(2,1)} %get-tuple-element.10), channel_id=1, source_target_pairs={{0,2},{2,4},{4,6},{6,0},{1,3},{3,5},{5,7},{7,1},{8,10},{10,12},{12... | collective-permute-start | bytes 466952 | tf_op jit(solution)/shard_map/ppermute | solution.py:124
  34.2 2.5 %collective-permute-start.1 = (bf16[304,256]{1,0:T(8,128)(2,1)}, bf16[304,256]{1,0:T(8,128)(2,1)S(1)}, u32[]{:S(2)}, u32[]{:S(2)}) collective-permute-start(bf16[304,256]{1,0:T(8,128)(2,1)} %get-tuple-element.11), channel_id=1, source_target_pairs={{0,6},{2,0},{4,2},{6,4},{1,7},{3,1},{5,3},{7,5},{8,14},{10,8},{12,... | collective-permute-start | bytes 466952 | tf_op jit(solution)/shard_map/ppermute | solution.py:124
  36.7 1.0 %select_select_fusion.3 = bf16[256,256]{1,0:T(8,128)(2,1)S(1)} fusion(bf16[256,256]{1,0:T(8,128)(2,1)S(1)} %collective-permute-done.6, bf16[256,256]{1,0:T(8,128)(2,1)S(1)} %collective-permute-done.7, bf16[256,256]{1,0:T(8,128)(2,1)S(1)} %collective-permute-done.8, bf16[256,256]{1,0:T(8,128)(2,1)S(1)} %collective-permute-done.5, ...), kind=kLoop, calls=%fused_computation.4 | loop fusion | flops 458752 | bytes 1179655 | tf_op jit(solution)/shard_map/jit(_where)/select_n | solution.py:108
  37.7 1.3 %collective-permute-start.12 = (bf16[256,256]{1,0:T(8,128)(2,1)S(1)}, bf16[256,256]{1,0:T(8,128)(2,1)S(1)}, u32[]{:S(2)}, u32[]{:S(2)}) collective-permute-start(bf16[256,256]{1,0:T(8,128)(2,1)S(1)} %select_select_fusion.3), channel_id=1, source_target_pairs={{0,96},{32,0},{64,32},{96,64},{1,97},{33,1},{65,33},{97,65},{2,98}... | collective-permute-start | bytes 393224 | tf_op jit(solution)/shard_map/ppermute | solution.py:133
  39.1 0.8 %collective-permute-start.14 = (bf16[256,256]{1,0:T(8,128)(2,1)S(1)}, bf16[256,256]{1,0:T(8,128)(2,1)S(1)}, u32[]{:S(2)}, u32[]{:S(2)}) collective-permute-start(bf16[256,256]{1,0:T(8,128)(2,1)S(1)} %select_select_fusion.2), channel_id=1, source_target_pairs={{0,64},{32,96},{64,0},{96,32},{1,65},{33,97},{65,1},{97,33},{2,66}... | collective-permute-start | bytes 393224 | tf_op jit(solution)/shard_map/ppermute | solution.py:133
  40.0 0.7 collective-permute-start.16
  40.7 7.5 %collective-permute-done.2 = bf16[304,256]{1,0:T(8,128)(2,1)S(1)} collective-permute-done((bf16[304,256]{1,0:T(8,128)(2,1)}, bf16[304,256]{1,0:T(8,128)(2,1)S(1)}, u32[]{:S(2)}, u32[]{:S(2)}) %collective-permute-start.2) | collective-permute-done | bytes 155680 | tf_op jit(solution)/shard_map/ppermute | solution.py:124
  48.3 3.4 %collective-permute-start.3 = (bf16[4,304,256]{2,1,0:T(8,128)(2,1)S(1)}, bf16[4,304,256]{2,1,0:T(8,128)(2,1)S(1)}, u32[]{:S(2)}, u32[]{:S(2)}) collective-permute-start(bf16[4,304,256]{2,1,0:T(8,128)(2,1)S(1)} %pad_maximum_fusion.refs_0_), channel_id=1, source_target_pairs={{0,1},{1,0},{2,3},{3,2},{4,5},{5,4},{6,7},{7,6},{8,9},{9,8},{10,11... | collective-permute-start | bytes 1867784 | tf_op jit(solution)/shard_map/ppermute | solution.py:126
  52.7 1.4 %collective-permute-start.18 = (bf16[256,256]{1,0:T(8,128)(2,1)S(1)}, bf16[256,256]{1,0:T(8,128)(2,1)S(1)}, u32[]{:S(2)}, u32[]{:S(2)}) collective-permute-start(bf16[256,256]{1,0:T(8,128)(2,1)S(1)} %select_select_fusion.refs_2_), channel_id=1, source_target_pairs={{0,6},{2,0},{4,2},{6,4},{1,7},{3,1},{5,3},{7,5},{8,14},{10,8},{12,... | collective-permute-start | bytes 393224 | tf_op jit(solution)/shard_map/ppermute | solution.py:136
  54.1 0.2 collective-permute-start.17
  54.3 4.5 %collective-permute-start.20 = (bf16[256,256]{1,0:T(8,128)(2,1)S(1)}, bf16[256,256]{1,0:T(8,128)(2,1)S(1)}, u32[]{:S(2)}, u32[]{:S(2)}) collective-permute-start(bf16[256,256]{1,0:T(8,128)(2,1)S(1)} %select_select_fusion.refs_2_), channel_id=1, source_target_pairs={{0,1},{1,0},{2,3},{3,2},{4,5},{5,4},{6,7},{7,6},{8,9},{9,8},{10,11... | collective-permute-start | bytes 393224 | tf_op jit(solution)/shard_map/ppermute | solution.py:137
  58.8 6.5 %collective-permute-start.23 = (bf16[256,256]{1,0:T(8,128)(2,1)S(1)}, bf16[256,256]{1,0:T(8,128)(2,1)S(1)}, u32[]{:S(2)}, u32[]{:S(2)}) collective-permute-start(bf16[256,256]{1,0:T(8,128)(2,1)S(1)} %collective-permute-done.19.refs_5_), channel_id=1, source_target_pairs={{0,1},{1,0},{2,3},{3,2},{4,5},{5,4},{6,7},{7,6},{8,9},{9,8},{10,11... | collective-permute-start | bytes 393224 | tf_op jit(solution)/shard_map/ppermute | solution.py:137
  65.4 0.4 collective-permute-start.21
  65.9 0.5 collective-permute-done.23.refs_9_
  66.3 0.4 collective-permute-done.22.refs_8_
  67.0 0.4 copy-done.10
  67.3 0.2 copy-done.11
  67.5 0.3 copy-done.2
  67.8 6.8 %shard_map.38 = f32[12,2,128,128]{3,2,1,0:T(8,128)} custom-call(s32[1]{0:T(128)} %bitcast.core_ref, bf16[4,304,256]{2,1,0:T(8,128)(2,1)} %copy-done.1, bf16[4,304,256]{2,1,0:T(8,128)(2,1)} %copy-done.2, bf16[256,256]{1,0:T(8,128)(2,1)} %copy-done.3, bf16[256,256]{1,0:T(8,128)(2,1)} %copy-done.7, bf16[256,256]{1,0:T(8,128)(2,1)} %copy-done.6, ...), custom_call_target="tpu_custom_call" | custom-call | tf_op jit(solution)/shard_map/pallas_call | solution.py:87
  (48 shorter events, 0.8 us)
Async XLA Ops:
  0.0 39.1 %copy-start = (bf16[1,2,128,256]{3,2,1,0:T(8,128)(2,1)S(1)}, bf16[1,2,128,256]{3,2,1,0:T(8,128)(2,1)}, u32[]{:S(2)}) copy-start(bf16[1,2,128,256]{3,2,1,0:T(8,128)(2,1)} %param.3) | copy-start | bytes 393220
  0.0 16.9 %collective-permute-start.5 = (bf16[256,256]{1,0:T(8,128)(2,1)}, bf16[256,256]{1,0:T(8,128)(2,1)S(1)}, u32[]{:S(2)}, u32[]{:S(2)}) collective-permute-start(bf16[256,256]{1,0:T(8,128)(2,1)} %bitcast.22), channel_id=1, source_target_pairs={{0,128},{128,0},{1,129},{129,1},{2,130},{130,2},{3,131},{131,3},{4... | collective-permute-start | bytes 393224 | tf_op jit(solution)/shard_map/ppermute | solution.py:118
  7.7 12.3 %collective-permute-start.11 = (bf16[256,256]{1,0:T(8,128)(2,1)}, bf16[256,256]{1,0:T(8,128)(2,1)S(1)}, u32[]{:S(2)}, u32[]{:S(2)}) collective-permute-start(bf16[256,256]{1,0:T(8,128)(2,1)} %bitcast.23), channel_id=1, source_target_pairs={{0,8},{8,16},{16,24},{24,0},{1,9},{9,17},{17,25},{25,1},{2,10},{10... | collective-permute-start | bytes 393224 | tf_op jit(solution)/shard_map/ppermute | solution.py:119
  9.0 5.3 %collective-permute-start.4 = (s32[1]{0:T(128)}, s32[1]{0:T(128)}, u32[]{:S(2)}, u32[]{:S(2)}) collective-permute-start(s32[1]{0:T(128)} %param.5), channel_id=1, source_target_pairs={{0,32},{32,64},{64,96},{96,0},{1,33},{33,65},{65,97},{97,1},{2,34}... | collective-permute-start | bytes 20 | tf_op jit(solution)/shard_map/ppermute | solution.py:121
  10.2 5.2 %collective-permute-start.15 = (s32[1]{0:T(128)}, s32[1]{0:T(128)}, u32[]{:S(2)}, u32[]{:S(2)}) collective-permute-start(s32[1]{0:T(128)} %param.5), channel_id=1, source_target_pairs={{0,96},{32,0},{64,32},{96,64},{1,97},{33,1},{65,33},{97,65},{2,98}... | collective-permute-start | bytes 20 | tf_op jit(solution)/shard_map/ppermute | solution.py:121
  11.7 21.6 %collective-permute-start.10 = (bf16[256,256]{1,0:T(8,128)(2,1)}, bf16[256,256]{1,0:T(8,128)(2,1)S(1)}, u32[]{:S(2)}, u32[]{:S(2)}) collective-permute-start(bf16[256,256]{1,0:T(8,128)(2,1)} %bitcast.24), channel_id=1, source_target_pairs={{0,16},{8,24},{16,0},{24,8},{1,17},{9,25},{17,1},{25,9},{2,18},{10... | collective-permute-start | bytes 393224 | tf_op jit(solution)/shard_map/ppermute | solution.py:119
  14.3 19.8 %collective-permute-start.9 = (bf16[256,256]{1,0:T(8,128)(2,1)}, bf16[256,256]{1,0:T(8,128)(2,1)S(1)}, u32[]{:S(2)}, u32[]{:S(2)}) collective-permute-start(bf16[256,256]{1,0:T(8,128)(2,1)} %bitcast.25), channel_id=1, source_target_pairs={{0,24},{8,0},{16,8},{24,16},{1,25},{9,1},{17,9},{25,17},{2,26},{10... | collective-permute-start | bytes 393224 | tf_op jit(solution)/shard_map/ppermute | solution.py:119
  15.4 4.4 %collective-permute-start.13 = (s32[1]{0:T(128)}, s32[1]{0:T(128)}, u32[]{:S(2)}, u32[]{:S(2)}) collective-permute-start(s32[1]{0:T(128)} %param.5), channel_id=1, source_target_pairs={{0,64},{32,96},{64,0},{96,32},{1,65},{33,97},{65,1},{97,33},{2,66}... | collective-permute-start | bytes 20 | tf_op jit(solution)/shard_map/ppermute | solution.py:121
  16.9 19.8 %collective-permute-start.8 = (bf16[256,256]{1,0:T(8,128)(2,1)S(1)}, bf16[256,256]{1,0:T(8,128)(2,1)S(1)}, u32[]{:S(2)}, u32[]{:S(2)}) collective-permute-start(bf16[256,256]{1,0:T(8,128)(2,1)S(1)} %collective-permute-done.5), channel_id=1, source_target_pairs={{0,8},{8,16},{16,24},{24,0},{1,9},{9,17},{17,25},{25,1},{2,10},{10... | collective-permute-start | bytes 393224 | tf_op jit(solution)/shard_map/ppermute | solution.py:120
  19.8 17.0 %collective-permute-start.7 = (bf16[256,256]{1,0:T(8,128)(2,1)S(1)}, bf16[256,256]{1,0:T(8,128)(2,1)S(1)}, u32[]{:S(2)}, u32[]{:S(2)}) collective-permute-start(bf16[256,256]{1,0:T(8,128)(2,1)S(1)} %collective-permute-done.5), channel_id=1, source_target_pairs={{0,16},{8,24},{16,0},{24,8},{1,17},{9,25},{17,1},{25,9},{2,18},{10... | collective-permute-start | bytes 393224 | tf_op jit(solution)/shard_map/ppermute | solution.py:120
  20.0 16.7 %collective-permute-start.6 = (bf16[256,256]{1,0:T(8,128)(2,1)S(1)}, bf16[256,256]{1,0:T(8,128)(2,1)S(1)}, u32[]{:S(2)}, u32[]{:S(2)}) collective-permute-start(bf16[256,256]{1,0:T(8,128)(2,1)S(1)} %collective-permute-done.5), channel_id=1, source_target_pairs={{0,24},{8,0},{16,8},{24,16},{1,25},{9,1},{17,9},{25,17},{2,26},{10... | collective-permute-start | bytes 393224 | tf_op jit(solution)/shard_map/ppermute | solution.py:120
  33.4 6.7 %collective-permute-start = (bf16[304,256]{1,0:T(8,128)(2,1)}, bf16[304,256]{1,0:T(8,128)(2,1)S(1)}, u32[]{:S(2)}, u32[]{:S(2)}) collective-permute-start(bf16[304,256]{1,0:T(8,128)(2,1)} %get-tuple-element.10), channel_id=1, source_target_pairs={{0,2},{2,4},{4,6},{6,0},{1,3},{3,5},{5,7},{7,1},{8,10},{10,12},{12... | collective-permute-start | bytes 466952 | tf_op jit(solution)/shard_map/ppermute | solution.py:124
  34.2 6.5 %collective-permute-start.1 = (bf16[304,256]{1,0:T(8,128)(2,1)}, bf16[304,256]{1,0:T(8,128)(2,1)S(1)}, u32[]{:S(2)}, u32[]{:S(2)}) collective-permute-start(bf16[304,256]{1,0:T(8,128)(2,1)} %get-tuple-element.11), channel_id=1, source_target_pairs={{0,6},{2,0},{4,2},{6,4},{1,7},{3,1},{5,3},{7,5},{8,14},{10,8},{12,... | collective-permute-start | bytes 466952 | tf_op jit(solution)/shard_map/ppermute | solution.py:124
  36.7 11.5 %copy-start.4 = (bf16[304,256]{1,0:T(8,128)(2,1)S(1)}, bf16[304,256]{1,0:T(8,128)(2,1)}, u32[]{:S(2)}) copy-start(bf16[304,256]{1,0:T(8,128)(2,1)} %get-tuple-element.9) | copy-start | bytes 466948
  36.7 11.5 %collective-permute-start.2 = (bf16[304,256]{1,0:T(8,128)(2,1)}, bf16[304,256]{1,0:T(8,128)(2,1)S(1)}, u32[]{:S(2)}, u32[]{:S(2)}) collective-permute-start(bf16[304,256]{1,0:T(8,128)(2,1)} %get-tuple-element.12), channel_id=1, source_target_pairs={{0,4},{2,6},{4,0},{6,2},{1,5},{3,7},{5,1},{7,3},{8,12},{10,14},{12... | collective-permute-start | bytes 466952 | tf_op jit(solution)/shard_map/ppermute | solution.py:124
  37.7 14.7 %collective-permute-start.12 = (bf16[256,256]{1,0:T(8,128)(2,1)S(1)}, bf16[256,256]{1,0:T(8,128)(2,1)S(1)}, u32[]{:S(2)}, u32[]{:S(2)}) collective-permute-start(bf16[256,256]{1,0:T(8,128)(2,1)S(1)} %select_select_fusion.3), channel_id=1, source_target_pairs={{0,96},{32,0},{64,32},{96,64},{1,97},{33,1},{65,33},{97,65},{2,98}... | collective-permute-start | bytes 393224 | tf_op jit(solution)/shard_map/ppermute | solution.py:133
  39.1 13.3 %collective-permute-start.14 = (bf16[256,256]{1,0:T(8,128)(2,1)S(1)}, bf16[256,256]{1,0:T(8,128)(2,1)S(1)}, u32[]{:S(2)}, u32[]{:S(2)}) collective-permute-start(bf16[256,256]{1,0:T(8,128)(2,1)S(1)} %select_select_fusion.2), channel_id=1, source_target_pairs={{0,64},{32,96},{64,0},{96,32},{1,65},{33,97},{65,1},{97,33},{2,66}... | collective-permute-start | bytes 393224 | tf_op jit(solution)/shard_map/ppermute | solution.py:133
  40.0 12.5 %collective-permute-start.16 = (bf16[256,256]{1,0:T(8,128)(2,1)S(1)}, bf16[256,256]{1,0:T(8,128)(2,1)S(1)}, u32[]{:S(2)}, u32[]{:S(2)}) collective-permute-start(bf16[256,256]{1,0:T(8,128)(2,1)S(1)} %select_select_fusion.1), channel_id=1, source_target_pairs={{0,32},{32,64},{64,96},{96,0},{1,33},{33,65},{65,97},{97,1},{2,34}... | collective-permute-start | bytes 393224 | tf_op jit(solution)/shard_map/ppermute | solution.py:133
  48.3 18.6 %copy-start.1 = (bf16[4,304,256]{2,1,0:T(8,128)(2,1)}, bf16[4,304,256]{2,1,0:T(8,128)(2,1)S(1)}, u32[]{:S(2)}) copy-start(bf16[4,304,256]{2,1,0:T(8,128)(2,1)S(1)} %pad_maximum_fusion.refs_0_) | copy-start | bytes 1867780
  48.3 18.6 %collective-permute-start.3 = (bf16[4,304,256]{2,1,0:T(8,128)(2,1)S(1)}, bf16[4,304,256]{2,1,0:T(8,128)(2,1)S(1)}, u32[]{:S(2)}, u32[]{:S(2)}) collective-permute-start(bf16[4,304,256]{2,1,0:T(8,128)(2,1)S(1)} %pad_maximum_fusion.refs_0_), channel_id=1, source_target_pairs={{0,1},{1,0},{2,3},{3,2},{4,5},{5,4},{6,7},{7,6},{8,9},{9,8},{10,11... | collective-permute-start | bytes 1867784 | tf_op jit(solution)/shard_map/ppermute | solution.py:126
  52.6 14.3 %copy-start.3 = (bf16[256,256]{1,0:T(8,128)(2,1)}, bf16[256,256]{1,0:T(8,128)(2,1)S(1)}, u32[]{:S(2)}) copy-start(bf16[256,256]{1,0:T(8,128)(2,1)S(1)} %select_select_fusion.refs_2_) | copy-start | bytes 393220
  52.6 6.2 %collective-permute-start.19 = (bf16[256,256]{1,0:T(8,128)(2,1)S(1)}, bf16[256,256]{1,0:T(8,128)(2,1)S(1)}, u32[]{:S(2)}, u32[]{:S(2)}) collective-permute-start(bf16[256,256]{1,0:T(8,128)(2,1)S(1)} %select_select_fusion.refs_2_), channel_id=1, source_target_pairs={{0,4},{2,6},{4,0},{6,2},{1,5},{3,7},{5,1},{7,3},{8,12},{10,14},{12... | collective-permute-start | bytes 393224 | tf_op jit(solution)/shard_map/ppermute | solution.py:136
  52.7 12.6 %collective-permute-start.18 = (bf16[256,256]{1,0:T(8,128)(2,1)S(1)}, bf16[256,256]{1,0:T(8,128)(2,1)S(1)}, u32[]{:S(2)}, u32[]{:S(2)}) collective-permute-start(bf16[256,256]{1,0:T(8,128)(2,1)S(1)} %select_select_fusion.refs_2_), channel_id=1, source_target_pairs={{0,6},{2,0},{4,2},{6,4},{1,7},{3,1},{5,3},{7,5},{8,14},{10,8},{12,... | collective-permute-start | bytes 393224 | tf_op jit(solution)/shard_map/ppermute | solution.py:136
  54.1 11.3 %collective-permute-start.17 = (bf16[256,256]{1,0:T(8,128)(2,1)S(1)}, bf16[256,256]{1,0:T(8,128)(2,1)S(1)}, u32[]{:S(2)}, u32[]{:S(2)}) collective-permute-start(bf16[256,256]{1,0:T(8,128)(2,1)S(1)} %select_select_fusion.refs_2_), channel_id=1, source_target_pairs={{0,2},{2,4},{4,6},{6,0},{1,3},{3,5},{5,7},{7,1},{8,10},{10,12},{12... | collective-permute-start | bytes 393224 | tf_op jit(solution)/shard_map/ppermute | solution.py:136
  54.3 11.5 %collective-permute-start.20 = (bf16[256,256]{1,0:T(8,128)(2,1)S(1)}, bf16[256,256]{1,0:T(8,128)(2,1)S(1)}, u32[]{:S(2)}, u32[]{:S(2)}) collective-permute-start(bf16[256,256]{1,0:T(8,128)(2,1)S(1)} %select_select_fusion.refs_2_), channel_id=1, source_target_pairs={{0,1},{1,0},{2,3},{3,2},{4,5},{5,4},{6,7},{7,6},{8,9},{9,8},{10,11... | collective-permute-start | bytes 393224 | tf_op jit(solution)/shard_map/ppermute | solution.py:137
  58.8 8.1 %copy-start.5 = (bf16[256,256]{1,0:T(8,128)(2,1)}, bf16[256,256]{1,0:T(8,128)(2,1)S(1)}, u32[]{:S(2)}) copy-start(bf16[256,256]{1,0:T(8,128)(2,1)S(1)} %collective-permute-done.19.refs_5_) | copy-start | bytes 393220
  58.8 7.5 %collective-permute-start.23 = (bf16[256,256]{1,0:T(8,128)(2,1)S(1)}, bf16[256,256]{1,0:T(8,128)(2,1)S(1)}, u32[]{:S(2)}, u32[]{:S(2)}) collective-permute-start(bf16[256,256]{1,0:T(8,128)(2,1)S(1)} %collective-permute-done.19.refs_5_), channel_id=1, source_target_pairs={{0,1},{1,0},{2,3},{3,2},{4,5},{5,4},{6,7},{7,6},{8,9},{9,8},{10,11... | collective-permute-start | bytes 393224 | tf_op jit(solution)/shard_map/ppermute | solution.py:137
  65.3 1.6 %copy-start.6 = (bf16[256,256]{1,0:T(8,128)(2,1)}, bf16[256,256]{1,0:T(8,128)(2,1)S(1)}, u32[]{:S(2)}) copy-start(bf16[256,256]{1,0:T(8,128)(2,1)S(1)} %collective-permute-done.18.refs_4_) | copy-start | bytes 393220
  65.3 1.3 %collective-permute-start.22 = (bf16[256,256]{1,0:T(8,128)(2,1)S(1)}, bf16[256,256]{1,0:T(8,128)(2,1)S(1)}, u32[]{:S(2)}, u32[]{:S(2)}) collective-permute-start(bf16[256,256]{1,0:T(8,128)(2,1)S(1)} %collective-permute-done.18.refs_4_), channel_id=1, source_target_pairs={{0,1},{1,0},{2,3},{3,2},{4,5},{5,4},{6,7},{7,6},{8,9},{9,8},{10,11... | collective-permute-start | bytes 393224 | tf_op jit(solution)/shard_map/ppermute | solution.py:137
  65.4 1.5 %copy-start.7 = (bf16[256,256]{1,0:T(8,128)(2,1)}, bf16[256,256]{1,0:T(8,128)(2,1)S(1)}, u32[]{:S(2)}) copy-start(bf16[256,256]{1,0:T(8,128)(2,1)S(1)} %collective-permute-done.17.refs_3_) | copy-start | bytes 393220
  65.4 1.4 %collective-permute-start.21 = (bf16[256,256]{1,0:T(8,128)(2,1)S(1)}, bf16[256,256]{1,0:T(8,128)(2,1)S(1)}, u32[]{:S(2)}, u32[]{:S(2)}) collective-permute-start(bf16[256,256]{1,0:T(8,128)(2,1)S(1)} %collective-permute-done.17.refs_3_), channel_id=1, source_target_pairs={{0,1},{1,0},{2,3},{3,2},{4,5},{5,4},{6,7},{7,6},{8,9},{9,8},{10,11... | collective-permute-start | bytes 393224 | tf_op jit(solution)/shard_map/ppermute | solution.py:137
  65.9 1.1 %copy-start.8 = (bf16[256,256]{1,0:T(8,128)(2,1)}, bf16[256,256]{1,0:T(8,128)(2,1)S(1)}, u32[]{:S(2)}) copy-start(bf16[256,256]{1,0:T(8,128)(2,1)S(1)} %collective-permute-done.20.refs_6_) | copy-start | bytes 393220
  (4 other events, 2.9 us)

commit v3 on v2

v3 whole, which is shorter than its diff:
```python
import jax
import jax.numpy as jnp
from jax import lax
from jax.experimental import pallas as pl
from jax.experimental.pallas import tpu as pltpu
from jax.sharding import Mesh
from jax.sharding import PartitionSpec as P

KA = ("zh", "x", "y")
GA = ("zl", "c")
XY = ("x", "y")
SWAP = [(0, 1), (1, 0)]
MIRROR = [(z, 7 - z) for z in range(8)]
STEPS = (0, 1, 3, 2)
TAG = 8
IN_SMEM = pl.BlockSpec(memory_space=pltpu.SMEM)
IN_VMEM = pl.BlockSpec(memory_space=pltpu.VMEM)


def ring(step, size=4):
    return [(i, (i + step) % size) for i in range(size)]


def pack_lines(slab, potential):
    rows, cells = slab.shape
    modes = potential.shape[0] // 4

    def kernel(slab_ref, pot_ref, *outs):
        zl = lax.axis_index("zl")
        for s, out in zip(STEPS, outs):
            out[:rows] = slab_ref[...]
            first = modes * lax.rem(zl + s, 4)
            for m in range(modes):
                out[rows + 2 * m : rows + 2 * m + 2] = pot_ref[first + m]

    return pl.pallas_call(
        kernel,
        in_specs=[IN_VMEM, IN_VMEM],
        out_shape=[jax.ShapeDtypeStruct((rows + 2 * modes, cells), slab.dtype)] * 4,
    )(slab, potential)


def pack_spread(slab, swapped, kq):
    rows, cells = slab.shape
    piece = rows // 16

    def kernel(kq_ref, slab_ref, swapped_ref, out):
        tag = jnp.full((TAG, cells), kq_ref[0].astype(jnp.float32)).astype(slab.dtype)
        for j in range(16):
            out[j, :piece] = slab_ref[j * piece : (j + 1) * piece]
            out[j, piece : 2 * piece] = swapped_ref[j * piece : (j + 1) * piece]
            out[j, 2 * piece :] = tag

    return pl.pallas_call(
        kernel,
        in_specs=[IN_SMEM, IN_VMEM, IN_VMEM],
        out_shape=jax.ShapeDtypeStruct((16, 2 * piece + TAG, cells), slab.dtype),
    )(kq, slab, swapped)


def choose(pieces):
    count, rows, cells = pieces.shape
    piece = (rows - TAG) // 2

    def kernel(ref, out):
        zh = lax.axis_index("zh")
        for d in range(count):
            source = jnp.max(ref[d, 2 * piece :, :128].astype(jnp.float32)).astype(jnp.int32)
            side = jnp.where(source // count == zh, 0, piece)
            out[d] = ref[lax.rem(source, count), pl.ds(pl.multiple_of(side, piece), piece), :]

    return pl.pallas_call(
        kernel,
        in_specs=[IN_VMEM],
        out_shape=jax.ShapeDtypeStruct((count, piece, cells), pieces.dtype),
    )(pieces)


def couple(kq, lines, twins, others, bands, modes, per_step):
    parts = len(others)
    half = parts // 2
    cells = others[0].shape[1]
    wide = parts * cells
    rows = 2 * bands
    share = lines.shape[1] - rows

    def kernel(kq_ref, lines_ref, twins_ref, *refs):
        other_refs = refs[:parts]
        out_ref = refs[parts]
        wave_re, wave_im, pots, left, right_a, right_b = refs[parts + 1 :]
        step = pl.program_id(0)
        first = lax.axis_index("c") * (share // 2)

        def fill(mode, right):
            for p in range(parts):
                at = slice(p * cells, (p + 1) * cells)
                dv_re = pots[pl.ds(first + 2 * mode, 1), at]
                dv_im = pots[pl.ds(first + 2 * mode + 1, 1), at]
                w_re, w_im = wave_re[:, at], wave_im[:, at]
                right[:bands, at] = (dv_re * w_re - dv_im * w_im).astype(jnp.bfloat16)
                right[bands:, at] = (dv_re * w_im + dv_im * w_re).astype(jnp.bfloat16)

        def finish(slot, right):
            full = lax.dot_general(left[...], right[...], (((1,), (1,)), ((), ())), preferred_element_type=jnp.float32)
            out_ref[slot, 0] = full[:bands, :bands] + full[bands:, bands:]
            out_ref[slot, 1] = full[:bands, bands:] - full[bands:, :bands]

        @pl.when(step == 0)
        def _():
            zl = lax.axis_index("zl")
            crossed = kq_ref[0] // 16 != lax.axis_index("zh")
            for p in range(parts):
                at = slice(p * cells, (p + 1) * cells)
                s = STEPS[p % half]
                turned = lax.rem(2 * zl + 5 - s, 4)
                turned = jnp.where(turned == 2, 3, jnp.where(turned == 3, 2, turned))
                index = jnp.where(crossed, turned, p % half)
                source = lines_ref if p < half else twins_ref
                wave_re[:, at] = source[index, :bands].astype(jnp.float32)
                wave_im[:, at] = source[index, bands:rows].astype(jnp.float32)
                pots[:, at] = source[index, rows:].astype(jnp.float32)
                left[:, at] = other_refs[p][...]

        for j in range(0, per_step, 2):
            fill(step * per_step + j, right_a)
            fill(step * per_step + j + 1, right_b)
            finish(j, right_a)
            finish(j + 1, right_b)

    whole = lambda a: pl.BlockSpec(a.shape, lambda i: (0,) * a.ndim)
    return pl.pallas_call(
        kernel,
        grid=(modes // per_step,),
        in_specs=[IN_SMEM] + [whole(a) for a in (lines, twins, *others)],
        out_specs=pl.BlockSpec((per_step, 2, bands, bands), lambda i: (i, 0, 0, 0)),
        out_shape=jax.ShapeDtypeStruct((modes, 2, bands, bands), jnp.float32),
        scratch_shapes=[
            pltpu.VMEM((bands, wide), jnp.float32),
            pltpu.VMEM((bands, wide), jnp.float32),
            pltpu.VMEM((share, wide), jnp.float32),
            pltpu.VMEM((rows, wide), jnp.bfloat16),
            pltpu.VMEM((rows, wide), jnp.bfloat16),
            pltpu.VMEM((rows, wide), jnp.bfloat16),
        ],
        compiler_params=pltpu.CompilerParams(dimension_semantics=("arbitrary",)),
    )(kq, lines, twins, *others)


def body(psi, dvscf, kq_map):
    bands, cells = psi.shape[2], psi.shape[3]
    modes = dvscf.shape[0] // 8
    slab = psi.reshape(2 * bands, cells)

    swapped = lax.ppermute(slab, ("zh", "zl"), MIRROR)
    packs = pack_lines(slab, dvscf)
    lines = [packs[0]] + [lax.ppermute(packs[i], "zl", ring(STEPS[i])) for i in (1, 2, 3)]
    lines = jnp.stack(lines)
    twins = lax.ppermute(lines, "c", SWAP)

    pieces = pack_spread(slab, swapped, kq_map)
    pieces = lax.all_to_all(pieces, XY, 0, 0, tiled=True)
    phi = lax.all_to_all(choose(pieces), XY, 0, 0, tiled=True).reshape(2 * bands, cells)

    others = [phi] + [lax.ppermute(phi, "zl", ring(STEPS[i])) for i in (1, 2, 3)]
    others += [lax.ppermute(o, "c", SWAP) for o in others]
    out = couple(kq_map, lines, twins, others, bands, modes, 4)
    return out[:, None]


def solution(mesh):
    finer = Mesh(mesh.devices.reshape(2, 4, 4, 4, 2), KA + GA)
    in_specs = (P(KA, None, None, GA), P(None, None, GA), P(KA))
    out_specs = P(GA, KA, None, None, None)
    return jax.shard_map(body, mesh=finer, in_specs=in_specs, out_specs=out_specs, check_vma=False)
```

time: 74.8 us -> 76.4 us (1.021)
  blocking collectives: 0 us -> 10.4 us
  between operations: 8.56 us -> 0.81 us
  waiting for transfers between devices: 11 us -> 6.77 us
  Pallas kernels: 8.56 us -> 12.2 us
    all_to_all x0 -> x1, blocking collectives: none -> 10.4 us  [body(): lax.all_to_all(choose(pieces), XY, 0, 0, tiled=True)]
    ppermute x19 -> x7, waiting for transfers between devices: 9.98 us -> 2.04 us  [the longest x1 2.02 us: body(): swapped = lax.ppermute(slab, ('zh', 'zl'), MIRROR)]
    all_to_all x0 -> x1, starting transfers between devices: none -> 6.64 us  [body(): pieces = lax.all_to_all(pieces, XY, 0, 0, tiled=True)]
    ppermute x19 -> x7, starting transfers between devices: 27.8 us -> 22.8 us  [the longest x3 13.8 us: body(): lax.ppermute(phi, 'zl', ring(STEPS[i]))]
    all_to_all x0 -> x1, waiting for transfers between devices: none -> 3.8 us  [body(): pieces = lax.all_to_all(pieces, XY, 0, 0, tiled=True)]
    pallas_call x2 -> x4, Pallas kernels: 8.56 us -> 12.2 us  [the longest x1 6.76 us: couple(): pl.pallas_call(kernel, grid=(modes // per_step,), in_specs=[IN_SMEM] + [w...]
    reshape x1 -> x0, local copies, waits for them, and re-layouts: 1.57 us -> none  [body(): packs = pack(zl[None], slab, dvscf.reshape(-1, cells))]
    select_n x4 -> x0, other arithmetic: 1.2 us -> none  [pick(): out = jnp.where(number == i, choice, out)]
  transfers between devices with their start and end apart: 24 -> 13, of which waited for: 5 -> 3; matrix products, arithmetic and copies ran while one was open for 4% -> 1% of each run, Pallas kernels for 2% -> 5%
where the time goes in v3:
time: 76.4 us; the launch traced here: 76.1 us
  starting transfers between devices  42.9 us (56%)
  Pallas kernels  12.2 us (16%)
  blocking collectives  10.4 us (14%)
  waiting for transfers between devices  6.77 us (9%)
  local copies, waits for them, and re-layouts  2.05 us (3%)
  other arithmetic  0.99 us (1%)
  between operations  0.81 us (1%)
    ppermute x3, starting transfers between devices, body(): lax.ppermute(phi, 'zl', ring(STEPS[i]))  13.8 us
    ppermute x4, starting transfers between devices, body(): others += [lax.ppermute(o, 'c', SWAP) for o in others]  10.6 us
    all_to_all x1, blocking collectives, body(): lax.all_to_all(choose(pieces), XY, 0, 0, tiled=True)  10.4 us
    pallas_call x1, Pallas kernels, couple(): pl.pallas_call(kernel, grid=(modes // per_step,), in_specs=[IN_SMEM] + [w...  6.76 us
    all_to_all x1, starting transfers between devices, body(): pieces = lax.all_to_all(pieces, XY, 0, 0, tiled=True)  6.64 us
    ppermute x3, starting transfers between devices, body(): lax.ppermute(packs[i], 'zl', ring(STEPS[i]))  5.45 us
    all_to_all x1, waiting for transfers between devices, body(): pieces = lax.all_to_all(pieces, XY, 0, 0, tiled=True)  3.8 us
    ppermute x1, starting transfers between devices, body(): swapped = lax.ppermute(slab, ('zh', 'zl'), MIRROR)  3.58 us
  transfers between devices with their start and end apart: 13, of which 3 were waited for; matrix products, arithmetic and copies ran while one was open for 1% of the time, Pallas kernels for 5%

profile of v3, /device:TPU:1, one launch (start us, length us, event | category | flops | bytes accessed | tf_op | source)
XLA Modules:
  0.0 76.1 jit_solution(14285191916154795920)
XLA Ops:
  0.0 1.9 %shard_map.37 = (bf16[304,256]{1,0:T(8,128)(2,1)}, bf16[304,256]{1,0:T(8,128)(2,1)}, bf16[304,256]{1,0:T(8,128)(2,1)}, bf16[304,256]{1,0:T(8,128)(2,1)}) custom-call(bf16[256,256]{1,0:T(8,128)(2,1)} %bitcast.14, bf16[96,2,256]{2,1,0:T(2,128)(2,1)} %pot_ref.1), custom_call_target="tpu_custom_call" | custom-call | tf_op jit(solution)/shard_map/pallas_call | solution.py:36
  1.9 2.5 %collective-permute-start = (bf16[304,256]{1,0:T(8,128)(2,1)}, bf16[304,256]{1,0:T(8,128)(2,1)S(1)}, u32[]{:S(2)}, u32[]{:S(2)}) collective-permute-start(bf16[304,256]{1,0:T(8,128)(2,1)} %get-tuple-element.10), channel_id=1, source_target_pairs={{0,2},{2,4},{4,6},{6,0},{1,3},{3,5},{5,7},{7,1},{8,10},{10,12},{12... | collective-permute-start | bytes 466952 | tf_op jit(solution)/shard_map/ppermute | solution.py:156
  4.3 2.7 %collective-permute-start.1 = (bf16[304,256]{1,0:T(8,128)(2,1)}, bf16[304,256]{1,0:T(8,128)(2,1)S(1)}, u32[]{:S(2)}, u32[]{:S(2)}) collective-permute-start(bf16[304,256]{1,0:T(8,128)(2,1)} %get-tuple-element.11), channel_id=1, source_target_pairs={{0,6},{2,0},{4,2},{6,4},{1,7},{3,1},{5,3},{7,5},{8,14},{10,8},{12,... | collective-permute-start | bytes 466952 | tf_op jit(solution)/shard_map/ppermute | solution.py:156
  7.0 0.3 collective-permute-start.2
  7.3 3.6 %collective-permute-start.4 = (bf16[256,256]{1,0:T(8,128)(2,1)}, bf16[256,256]{1,0:T(8,128)(2,1)S(1)}, u32[]{:S(2)}, u32[]{:S(2)}) collective-permute-start(bf16[256,256]{1,0:T(8,128)(2,1)} %bitcast.15), channel_id=1, source_target_pairs={{0,134},{2,132},{4,130},{6,128},{128,6},{130,4},{132,2},{134,0},{1... | collective-permute-start | bytes 393224 | tf_op jit(solution)/shard_map/ppermute | solution.py:154
  11.6 2.0 %collective-permute-done.4.swapped_ref = bf16[256,256]{1,0:T(8,128)(2,1)S(1)} collective-permute-done((bf16[256,256]{1,0:T(8,128)(2,1)}, bf16[256,256]{1,0:T(8,128)(2,1)S(1)}, u32[]{:S(2)}, u32[]{:S(2)}) %collective-permute-start.4) | collective-permute-done | bytes 131104 | tf_op jit(solution)/shard_map/ppermute | solution.py:154
  13.6 0.6 copy-done.11
  14.2 1.7 %shard_map.38 = bf16[16,40,256]{2,1,0:T(8,128)(2,1)} custom-call(s32[1]{0:T(128)S(6)} %copy.5.kq_ref, bf16[256,256]{1,0:T(8,128)(2,1)} %bitcast.16, bf16[256,256]{1,0:T(8,128)(2,1)} %copy-done.11), custom_call_target="tpu_custom_call" | custom-call | tf_op jit(solution)/shard_map/pallas_call | solution.py:54
  15.9 6.6 %all-to-all-start = ((bf16[16,40,256]{2,1,0:T(8,128)(2,1)}), bf16[16,40,256]{2,1,0:T(8,128)(2,1)S(1)}, u32[]{:S(2)}, u32[]{:S(2)}) async-start(bf16[16,40,256]{2,1,0:T(8,128)(2,1)} %shard_map.38), calls=%async_computation | async-start | bytes 655360 | tf_op jit(solution)/shard_map/all_to_all | solution.py:161
  22.6 0.0 collective-permute-done
  22.6 0.0 collective-permute-done.1
  22.6 0.0 collective-permute-done.2
  22.6 1.0 %pad_maximum_fusion.lines_ref = bf16[4,304,256]{2,1,0:T(8,128)(2,1)S(1)} fusion(bf16[1,304,256]{2,1,0:T(8,128)(2,1)S(1)} %bitcast.20, bf16[1,304,256]{2,1,0:T(8,128)(2,1)S(1)} %bitcast.19, bf16[1,304,256]{2,1,0:T(8,128)(2,1)S(1)} %bitcast.18, bf16[1,304,256]{2,1,0:T(8,128)(2,1)} %bitcast.17), kind=kLoop, calls=%fused_computation | loop fusion | flops 933888 | bytes 1245184 | tf_op jit(solution)/shard_map/stack | solution.py:157
  23.6 2.9 %collective-permute-start.3 = (bf16[4,304,256]{2,1,0:T(8,128)(2,1)S(1)}, bf16[4,304,256]{2,1,0:T(8,128)(2,1)S(1)}, u32[]{:S(2)}, u32[]{:S(2)}) collective-permute-start(bf16[4,304,256]{2,1,0:T(8,128)(2,1)S(1)} %pad_maximum_fusion.lines_ref), channel_id=1, source_target_pairs={{0,1},{1,0},{2,3},{3,2},{4,5},{5,4},{6,7},{7,6},{8,9},{9,8},{10,11... | collective-permute-start | bytes 1867784 | tf_op jit(solution)/shard_map/ppermute | solution.py:158
  26.5 3.8 %all-to-all-done.ref = bf16[16,40,256]{2,1,0:T(8,128)(2,1)S(1)} async-done(((bf16[16,40,256]{2,1,0:T(8,128)(2,1)}), bf16[16,40,256]{2,1,0:T(8,128)(2,1)S(1)}, u32[]{:S(2)}, u32[]{:S(2)}) %all-to-all-start) | async-done | bytes 327712 | tf_op jit(solution)/shard_map/all_to_all | solution.py:161
  30.3 0.7 copy-done.1
  31.0 1.9 %shard_map.39 = bf16[16,16,256]{2,1,0:T(8,128)(2,1)} custom-call(bf16[16,40,256]{2,1,0:T(8,128)(2,1)} %copy-done.1), custom_call_target="tpu_custom_call" | custom-call | tf_op jit(solution)/shard_map/pallas_call | solution.py:72
  32.9 10.4 %all_to_all.10 = bf16[16,16,256]{2,1,0:T(8,128)(2,1)S(1)} all-to-all(bf16[16,16,256]{2,1,0:T(8,128)(2,1)} %shard_map.39), channel_id=1, replica_groups=mesh['zh'=2,'x'=4,'y'=4,'zl'=4,'c'=2] {'x','y'}, dimensions={0} | all-to-all | bytes 262144 | tf_op jit(solution)/shard_map/all_to_all | solution.py:162
  43.2 11.2 %collective-permute-start.7 = (bf16[256,256]{1,0:T(8,128)(2,1)S(1)}, bf16[256,256]{1,0:T(8,128)(2,1)S(1)}, u32[]{:S(2)}, u32[]{:S(2)}) collective-permute-start(bf16[256,256]{1,0:T(8,128)(2,1)S(1)} %bitcast.9), channel_id=1, source_target_pairs={{0,4},{2,6},{4,0},{6,2},{1,5},{3,7},{5,1},{7,3},{8,12},{10,14},{12... | collective-permute-start | bytes 393224 | tf_op jit(solution)/shard_map/ppermute | solution.py:164
  54.5 2.5 %collective-permute-start.6 = (bf16[256,256]{1,0:T(8,128)(2,1)S(1)}, bf16[256,256]{1,0:T(8,128)(2,1)S(1)}, u32[]{:S(2)}, u32[]{:S(2)}) collective-permute-start(bf16[256,256]{1,0:T(8,128)(2,1)S(1)} %bitcast.10), channel_id=1, source_target_pairs={{0,6},{2,0},{4,2},{6,4},{1,7},{3,1},{5,3},{7,5},{8,14},{10,8},{12,... | collective-permute-start | bytes 393224 | tf_op jit(solution)/shard_map/ppermute | solution.py:164
  57.0 0.0 collective-permute-start.5
  57.0 3.9 %collective-permute-start.8 = (bf16[256,256]{1,0:T(8,128)(2,1)S(1)}, bf16[256,256]{1,0:T(8,128)(2,1)S(1)}, u32[]{:S(2)}, u32[]{:S(2)}) collective-permute-start(bf16[256,256]{1,0:T(8,128)(2,1)S(1)} %bitcast.12), channel_id=1, source_target_pairs={{0,1},{1,0},{2,3},{3,2},{4,5},{5,4},{6,7},{7,6},{8,9},{9,8},{10,11... | collective-permute-start | bytes 393224 | tf_op jit(solution)/shard_map/ppermute | solution.py:165
  60.9 0.0 collective-permute-done.7.refs_3_
  60.9 1.3 %collective-permute-start.11 = (bf16[256,256]{1,0:T(8,128)(2,1)S(1)}, bf16[256,256]{1,0:T(8,128)(2,1)S(1)}, u32[]{:S(2)}, u32[]{:S(2)}) collective-permute-start(bf16[256,256]{1,0:T(8,128)(2,1)S(1)} %collective-permute-done.7.refs_3_), channel_id=1, source_target_pairs={{0,1},{1,0},{2,3},{3,2},{4,5},{5,4},{6,7},{7,6},{8,9},{9,8},{10,11... | collective-permute-start | bytes 393224 | tf_op jit(solution)/shard_map/ppermute | solution.py:165
  62.2 0.0 collective-permute-done.6.refs_2_
  62.2 2.7 %collective-permute-start.10 = (bf16[256,256]{1,0:T(8,128)(2,1)S(1)}, bf16[256,256]{1,0:T(8,128)(2,1)S(1)}, u32[]{:S(2)}, u32[]{:S(2)}) collective-permute-start(bf16[256,256]{1,0:T(8,128)(2,1)S(1)} %collective-permute-done.6.refs_2_), channel_id=1, source_target_pairs={{0,1},{1,0},{2,3},{3,2},{4,5},{5,4},{6,7},{7,6},{8,9},{9,8},{10,11... | collective-permute-start | bytes 393224 | tf_op jit(solution)/shard_map/ppermute | solution.py:165
  64.9 2.7 %collective-permute-start.9 = (bf16[256,256]{1,0:T(8,128)(2,1)S(1)}, bf16[256,256]{1,0:T(8,128)(2,1)S(1)}, u32[]{:S(2)}, u32[]{:S(2)}) collective-permute-start(bf16[256,256]{1,0:T(8,128)(2,1)S(1)} %collective-permute-done.5.refs_1_), channel_id=1, source_target_pairs={{0,1},{1,0},{2,3},{3,2},{4,5},{5,4},{6,7},{7,6},{8,9},{9,8},{10,11... | collective-permute-start | bytes 393224 | tf_op jit(solution)/shard_map/ppermute | solution.py:165
  67.6 0.0 collective-permute-done.3.twins_ref
  67.6 0.0 collective-permute-done.11.refs_7_
  67.7 0.9 %collective-permute-done.9.refs_5_ = bf16[256,256]{1,0:T(8,128)(2,1)S(1)} collective-permute-done((bf16[256,256]{1,0:T(8,128)(2,1)S(1)}, bf16[256,256]{1,0:T(8,128)(2,1)S(1)}, u32[]{:S(2)}, u32[]{:S(2)}) %collective-permute-start.9) | collective-permute-done | bytes 131104 | tf_op jit(solution)/shard_map/ppermute | solution.py:165
  68.7 0.6 copy-done.10
  69.3 6.8 %shard_map.40 = f32[12,2,128,128]{3,2,1,0:T(8,128)} custom-call(s32[1]{0:T(128)S(6)} %copy.5.kq_ref, bf16[4,304,256]{2,1,0:T(8,128)(2,1)} %copy-done, bf16[4,304,256]{2,1,0:T(8,128)(2,1)} %copy-done.2, bf16[256,256]{1,0:T(8,128)(2,1)} %bitcast.13, bf16[256,256]{1,0:T(8,128)(2,1)} %copy-done.6, bf16[256,256]{1,0:T(8,128)(2,1)} %copy-done.5, ...), custom_call_target="tpu_custom_call" | custom-call | tf_op jit(solution)/shard_map/pallas_call | solution.py:131
  (24 shorter events, 0.0 us)
Async XLA Ops:
  1.9 20.7 %collective-permute-start = (bf16[304,256]{1,0:T(8,128)(2,1)}, bf16[304,256]{1,0:T(8,128)(2,1)S(1)}, u32[]{:S(2)}, u32[]{:S(2)}) collective-permute-start(bf16[304,256]{1,0:T(8,128)(2,1)} %get-tuple-element.10), channel_id=1, source_target_pairs={{0,2},{2,4},{4,6},{6,0},{1,3},{3,5},{5,7},{7,1},{8,10},{10,12},{12... | collective-permute-start | bytes 466952 | tf_op jit(solution)/shard_map/ppermute | solution.py:156
  4.3 18.3 %collective-permute-start.1 = (bf16[304,256]{1,0:T(8,128)(2,1)}, bf16[304,256]{1,0:T(8,128)(2,1)S(1)}, u32[]{:S(2)}, u32[]{:S(2)}) collective-permute-start(bf16[304,256]{1,0:T(8,128)(2,1)} %get-tuple-element.11), channel_id=1, source_target_pairs={{0,6},{2,0},{4,2},{6,4},{1,7},{3,1},{5,3},{7,5},{8,14},{10,8},{12,... | collective-permute-start | bytes 466952 | tf_op jit(solution)/shard_map/ppermute | solution.py:156
  7.0 15.6 %collective-permute-start.2 = (bf16[304,256]{1,0:T(8,128)(2,1)}, bf16[304,256]{1,0:T(8,128)(2,1)S(1)}, u32[]{:S(2)}, u32[]{:S(2)}) collective-permute-start(bf16[304,256]{1,0:T(8,128)(2,1)} %get-tuple-element.12), channel_id=1, source_target_pairs={{0,4},{2,6},{4,0},{6,2},{1,5},{3,7},{5,1},{7,3},{8,12},{10,14},{12... | collective-permute-start | bytes 466952 | tf_op jit(solution)/shard_map/ppermute | solution.py:156
  7.3 6.3 %collective-permute-start.4 = (bf16[256,256]{1,0:T(8,128)(2,1)}, bf16[256,256]{1,0:T(8,128)(2,1)S(1)}, u32[]{:S(2)}, u32[]{:S(2)}) collective-permute-start(bf16[256,256]{1,0:T(8,128)(2,1)} %bitcast.15), channel_id=1, source_target_pairs={{0,134},{2,132},{4,130},{6,128},{128,6},{130,4},{132,2},{134,0},{1... | collective-permute-start | bytes 393224 | tf_op jit(solution)/shard_map/ppermute | solution.py:154
  13.6 0.7 copy-start.11
  15.9 14.3 %all-to-all-start = ((bf16[16,40,256]{2,1,0:T(8,128)(2,1)}), bf16[16,40,256]{2,1,0:T(8,128)(2,1)S(1)}, u32[]{:S(2)}, u32[]{:S(2)}) async-start(bf16[16,40,256]{2,1,0:T(8,128)(2,1)} %shard_map.38), calls=%async_computation | async-start | bytes 655360 | tf_op jit(solution)/shard_map/all_to_all | solution.py:161
  23.6 45.0 %copy-start = (bf16[4,304,256]{2,1,0:T(8,128)(2,1)}, bf16[4,304,256]{2,1,0:T(8,128)(2,1)S(1)}, u32[]{:S(2)}) copy-start(bf16[4,304,256]{2,1,0:T(8,128)(2,1)S(1)} %pad_maximum_fusion.lines_ref) | copy-start | bytes 1867780
  23.6 44.0 %collective-permute-start.3 = (bf16[4,304,256]{2,1,0:T(8,128)(2,1)S(1)}, bf16[4,304,256]{2,1,0:T(8,128)(2,1)S(1)}, u32[]{:S(2)}, u32[]{:S(2)}) collective-permute-start(bf16[4,304,256]{2,1,0:T(8,128)(2,1)S(1)} %pad_maximum_fusion.lines_ref), channel_id=1, source_target_pairs={{0,1},{1,0},{2,3},{3,2},{4,5},{5,4},{6,7},{7,6},{8,9},{9,8},{10,11... | collective-permute-start | bytes 1867784 | tf_op jit(solution)/shard_map/ppermute | solution.py:158
  30.3 0.7 copy-start.1
  43.2 25.4 %copy-start.3 = (bf16[16,16,256]{2,1,0:T(8,128)(2,1)}, bf16[16,16,256]{2,1,0:T(8,128)(2,1)S(1)}, u32[]{:S(2)}) copy-start(bf16[16,16,256]{2,1,0:T(8,128)(2,1)S(1)} %all_to_all.10) | copy-start | bytes 393220
  43.2 17.7 %collective-permute-start.7 = (bf16[256,256]{1,0:T(8,128)(2,1)S(1)}, bf16[256,256]{1,0:T(8,128)(2,1)S(1)}, u32[]{:S(2)}, u32[]{:S(2)}) collective-permute-start(bf16[256,256]{1,0:T(8,128)(2,1)S(1)} %bitcast.9), channel_id=1, source_target_pairs={{0,4},{2,6},{4,0},{6,2},{1,5},{3,7},{5,1},{7,3},{8,12},{10,14},{12... | collective-permute-start | bytes 393224 | tf_op jit(solution)/shard_map/ppermute | solution.py:164
  54.5 7.7 %collective-permute-start.6 = (bf16[256,256]{1,0:T(8,128)(2,1)S(1)}, bf16[256,256]{1,0:T(8,128)(2,1)S(1)}, u32[]{:S(2)}, u32[]{:S(2)}) collective-permute-start(bf16[256,256]{1,0:T(8,128)(2,1)S(1)} %bitcast.10), channel_id=1, source_target_pairs={{0,6},{2,0},{4,2},{6,4},{1,7},{3,1},{5,3},{7,5},{8,14},{10,8},{12,... | collective-permute-start | bytes 393224 | tf_op jit(solution)/shard_map/ppermute | solution.py:164
  57.0 7.9 %collective-permute-start.5 = (bf16[256,256]{1,0:T(8,128)(2,1)S(1)}, bf16[256,256]{1,0:T(8,128)(2,1)S(1)}, u32[]{:S(2)}, u32[]{:S(2)}) collective-permute-start(bf16[256,256]{1,0:T(8,128)(2,1)S(1)} %bitcast.11), channel_id=1, source_target_pairs={{0,2},{2,4},{4,6},{6,0},{1,3},{3,5},{5,7},{7,1},{8,10},{10,12},{12... | collective-permute-start | bytes 393224 | tf_op jit(solution)/shard_map/ppermute | solution.py:164
  57.0 10.6 %collective-permute-start.8 = (bf16[256,256]{1,0:T(8,128)(2,1)S(1)}, bf16[256,256]{1,0:T(8,128)(2,1)S(1)}, u32[]{:S(2)}, u32[]{:S(2)}) collective-permute-start(bf16[256,256]{1,0:T(8,128)(2,1)S(1)} %bitcast.12), channel_id=1, source_target_pairs={{0,1},{1,0},{2,3},{3,2},{4,5},{5,4},{6,7},{7,6},{8,9},{9,8},{10,11... | collective-permute-start | bytes 393224 | tf_op jit(solution)/shard_map/ppermute | solution.py:165
  60.9 7.7 %copy-start.4 = (bf16[256,256]{1,0:T(8,128)(2,1)}, bf16[256,256]{1,0:T(8,128)(2,1)S(1)}, u32[]{:S(2)}) copy-start(bf16[256,256]{1,0:T(8,128)(2,1)S(1)} %collective-permute-done.7.refs_3_) | copy-start | bytes 393220
  60.9 6.7 %collective-permute-start.11 = (bf16[256,256]{1,0:T(8,128)(2,1)S(1)}, bf16[256,256]{1,0:T(8,128)(2,1)S(1)}, u32[]{:S(2)}, u32[]{:S(2)}) collective-permute-start(bf16[256,256]{1,0:T(8,128)(2,1)S(1)} %collective-permute-done.7.refs_3_), channel_id=1, source_target_pairs={{0,1},{1,0},{2,3},{3,2},{4,5},{5,4},{6,7},{7,6},{8,9},{9,8},{10,11... | collective-permute-start | bytes 393224 | tf_op jit(solution)/shard_map/ppermute | solution.py:165
  62.2 6.4 %copy-start.5 = (bf16[256,256]{1,0:T(8,128)(2,1)}, bf16[256,256]{1,0:T(8,128)(2,1)S(1)}, u32[]{:S(2)}) copy-start(bf16[256,256]{1,0:T(8,128)(2,1)S(1)} %collective-permute-done.6.refs_2_) | copy-start | bytes 393220
  62.2 5.4 %collective-permute-start.10 = (bf16[256,256]{1,0:T(8,128)(2,1)S(1)}, bf16[256,256]{1,0:T(8,128)(2,1)S(1)}, u32[]{:S(2)}, u32[]{:S(2)}) collective-permute-start(bf16[256,256]{1,0:T(8,128)(2,1)S(1)} %collective-permute-done.6.refs_2_), channel_id=1, source_target_pairs={{0,1},{1,0},{2,3},{3,2},{4,5},{5,4},{6,7},{7,6},{8,9},{9,8},{10,11... | collective-permute-start | bytes 393224 | tf_op jit(solution)/shard_map/ppermute | solution.py:165
  64.9 3.7 %copy-start.6 = (bf16[256,256]{1,0:T(8,128)(2,1)}, bf16[256,256]{1,0:T(8,128)(2,1)S(1)}, u32[]{:S(2)}) copy-start(bf16[256,256]{1,0:T(8,128)(2,1)S(1)} %collective-permute-done.5.refs_1_) | copy-start | bytes 393220
  64.9 3.7 %collective-permute-start.9 = (bf16[256,256]{1,0:T(8,128)(2,1)S(1)}, bf16[256,256]{1,0:T(8,128)(2,1)S(1)}, u32[]{:S(2)}, u32[]{:S(2)}) collective-permute-start(bf16[256,256]{1,0:T(8,128)(2,1)S(1)} %collective-permute-done.5.refs_1_), channel_id=1, source_target_pairs={{0,1},{1,0},{2,3},{3,2},{4,5},{5,4},{6,7},{7,6},{8,9},{9,8},{10,11... | collective-permute-start | bytes 393224 | tf_op jit(solution)/shard_map/ppermute | solution.py:165
  67.6 1.0 %copy-start.7 = (bf16[256,256]{1,0:T(8,128)(2,1)}, bf16[256,256]{1,0:T(8,128)(2,1)S(1)}, u32[]{:S(2)}) copy-start(bf16[256,256]{1,0:T(8,128)(2,1)S(1)} %collective-permute-done.8.refs_4_) | copy-start | bytes 393220
  67.6 1.0 %copy-start.2 = (bf16[4,304,256]{2,1,0:T(8,128)(2,1)}, bf16[4,304,256]{2,1,0:T(8,128)(2,1)S(1)}, u32[]{:S(2)}) copy-start(bf16[4,304,256]{2,1,0:T(8,128)(2,1)S(1)} %collective-permute-done.3.twins_ref) | copy-start | bytes 1867780
  67.6 1.0 %copy-start.8 = (bf16[256,256]{1,0:T(8,128)(2,1)}, bf16[256,256]{1,0:T(8,128)(2,1)S(1)}, u32[]{:S(2)}) copy-start(bf16[256,256]{1,0:T(8,128)(2,1)S(1)} %collective-permute-done.11.refs_7_) | copy-start | bytes 393220
  67.7 1.0 %copy-start.9 = (bf16[256,256]{1,0:T(8,128)(2,1)}, bf16[256,256]{1,0:T(8,128)(2,1)S(1)}, u32[]{:S(2)}) copy-start(bf16[256,256]{1,0:T(8,128)(2,1)S(1)} %collective-permute-done.10.refs_6_) | copy-start | bytes 393220
  68.7 0.6 copy-start.10

commit v4 on v3

v4 whole, which is shorter than its diff:
```python
import jax
import jax.numpy as jnp
from jax import lax
from jax.experimental import pallas as pl
from jax.experimental.pallas import tpu as pltpu
from jax.sharding import Mesh
from jax.sharding import PartitionSpec as P

KA = ("zh", "x", "y")
GA = ("zl", "c")
XY = ("x", "y")
SWAP = [(0, 1), (1, 0)]
MIRROR = [(z, 7 - z) for z in range(8)]
STEPS = (0, 1, 3, 2)
TAG = 8
IN_SMEM = pl.BlockSpec(memory_space=pltpu.SMEM)
IN_VMEM = pl.BlockSpec(memory_space=pltpu.VMEM)


def ring(step, size=4):
    return [(i, (i + step) % size) for i in range(size)]


def send(value, axis, pairs):
    return lax.ppermute(value, axis, pairs)


def pack_lines(slab, potential):
    rows, cells = slab.shape
    modes = potential.shape[0] // 4

    def kernel(slab_ref, pot_ref, *outs):
        zl = lax.axis_index("zl")
        for s, out in zip(STEPS, outs):
            out[:rows] = slab_ref[...]
            first = modes * lax.rem(zl + s, 4)
            for m in range(modes):
                out[rows + 2 * m : rows + 2 * m + 2] = pot_ref[first + m]

    return pl.pallas_call(
        kernel,
        in_specs=[IN_VMEM, IN_VMEM],
        out_shape=[jax.ShapeDtypeStruct((rows + 2 * modes, cells), slab.dtype)] * 4,
    )(slab, potential)


def pack_spread(slab, kq):
    rows, cells = slab.shape
    piece = rows // 16

    def kernel(kq_ref, slab_ref, out):
        tag = jnp.full((TAG, cells), kq_ref[0].astype(jnp.float32)).astype(slab.dtype)
        for j in range(16):
            out[j, :piece] = slab_ref[j * piece : (j + 1) * piece]
            out[j, piece:] = tag

    return pl.pallas_call(
        kernel,
        in_specs=[IN_SMEM, IN_VMEM],
        out_shape=jax.ShapeDtypeStruct((16, piece + TAG, cells), slab.dtype),
    )(kq, slab)


def strip(tagged):
    count, rows, cells = tagged.shape

    def kernel(ref, out):
        out[...] = ref[:, : rows - TAG]

    return pl.pallas_call(
        kernel,
        in_specs=[IN_VMEM],
        out_shape=jax.ShapeDtypeStruct((count, rows - TAG, cells), tagged.dtype),
    )(tagged)


def choose(tagged, swapped):
    count, piece, _ = swapped.shape

    def kernel(ref, swapped_ref, out):
        zh = lax.axis_index("zh")
        for d in range(count):
            source = jnp.max(ref[d, piece:, :128].astype(jnp.float32)).astype(jnp.int32)
            block = lax.rem(source, count)
            here = source // count == zh

            @pl.when(here)
            def _():
                out[d] = ref[block, :piece]

            @pl.when(jnp.logical_not(here))
            def _():
                out[d] = swapped_ref[block]

    return pl.pallas_call(
        kernel,
        in_specs=[IN_VMEM, IN_VMEM],
        out_shape=jax.ShapeDtypeStruct(swapped.shape, swapped.dtype),
    )(tagged, swapped)


def couple(kq, lines, twins, others, bands, modes):
    parts = len(others)
    half = parts // 2
    cells = others[0].shape[1]
    wide = parts * cells
    rows = 2 * bands
    share = lines.shape[1] - rows

    def kernel(kq_ref, lines_ref, twins_ref, *refs):
        other_refs = refs[:parts]
        out_ref = refs[parts]
        wave_re, wave_im, pots, left, right_a, right_b, result, sems = refs[parts + 1 :]
        first = lax.axis_index("c") * (share // 2)
        zl = lax.axis_index("zl")
        crossed = kq_ref[0] // 16 != lax.axis_index("zh")
        for p in range(parts):
            at = slice(p * cells, (p + 1) * cells)
            s = STEPS[p % half]
            turned = lax.rem(2 * zl + 5 - s, 4)
            turned = jnp.where(turned == 2, 3, jnp.where(turned == 3, 2, turned))
            index = jnp.where(crossed, turned, p % half)
            source = lines_ref if p < half else twins_ref
            wave_re[:, at] = source[index, :bands].astype(jnp.float32)
            wave_im[:, at] = source[index, bands:rows].astype(jnp.float32)
            pots[:, at] = source[index, rows:].astype(jnp.float32)
            left[:, at] = other_refs[p][...]

        def fill(mode, right):
            for p in range(parts):
                at = slice(p * cells, (p + 1) * cells)
                dv_re = pots[pl.ds(first + 2 * mode, 1), at]
                dv_im = pots[pl.ds(first + 2 * mode + 1, 1), at]
                w_re, w_im = wave_re[:, at], wave_im[:, at]
                right[:bands, at] = (dv_re * w_re - dv_im * w_im).astype(jnp.bfloat16)
                right[bands:, at] = (dv_re * w_im + dv_im * w_re).astype(jnp.bfloat16)

        def finish(mode, right):
            full = lax.dot_general(left[...], right[...], (((1,), (1,)), ((), ())), preferred_element_type=jnp.float32)
            result[mode, 0] = full[:bands, :bands] + full[bands:, bands:]
            result[mode, 1] = full[:bands, bands:] - full[bands:, :bands]

        def copy(pair):
            return pltpu.make_async_copy(result.at[pl.ds(2 * pair, 2)], out_ref.at[pl.ds(2 * pair, 2)], sems.at[pair])

        fill(0, right_a)

        def pair_step(pair, carry):
            fill(2 * pair + 1, right_b)
            finish(2 * pair, right_a)
            fill(jnp.minimum(2 * pair + 2, modes - 1), right_a)
            finish(2 * pair + 1, right_b)
            copy(pair).start()
            return carry

        lax.fori_loop(0, modes // 2, pair_step, 0)
        for pair in range(modes // 2):
            copy(pair).wait()

    return pl.pallas_call(
        kernel,
        in_specs=[IN_SMEM] + [IN_VMEM] * (2 + parts),
        out_specs=pl.BlockSpec(memory_space=pl.ANY),
        out_shape=jax.ShapeDtypeStruct((modes, 2, bands, bands), jnp.float32),
        scratch_shapes=[
            pltpu.VMEM((bands, wide), jnp.float32),
            pltpu.VMEM((bands, wide), jnp.float32),
            pltpu.VMEM((share, wide), jnp.float32),
            pltpu.VMEM((rows, wide), jnp.bfloat16),
            pltpu.VMEM((rows, wide), jnp.bfloat16),
            pltpu.VMEM((rows, wide), jnp.bfloat16),
            pltpu.VMEM((modes, 2, bands, bands), jnp.float32),
            pltpu.SemaphoreType.DMA((modes // 2,)),
        ],
    )(kq, lines, twins, *others)


def body(psi, dvscf, kq_map):
    bands, cells = psi.shape[2], psi.shape[3]
    modes = dvscf.shape[0] // 8
    slab = psi.reshape(2 * bands, cells)

    tagged = pack_spread(slab, kq_map)
    tagged = lax.all_to_all(tagged, XY, 0, 0, tiled=True)
    swapped = send(strip(tagged), ("zh", "zl"), MIRROR)
    packs = pack_lines(slab, dvscf)
    lines = [packs[0]] + [send(packs[i], "zl", ring(STEPS[i])) for i in (1, 2, 3)]
    lines = jnp.stack(lines)
    twins = send(lines, "c", SWAP)
    chosen = choose(tagged, swapped)
    phi = lax.all_to_all(chosen, XY, 0, 0, tiled=True).reshape(2 * bands, cells)

    others = [phi] + [send(phi, "zl", ring(STEPS[i])) for i in (1, 2, 3)]
    others += [send(o, "c", SWAP) for o in others]
    out = couple(kq_map, lines, twins, others, bands, modes)
    return out[:, None]


def solution(mesh):
    finer = Mesh(mesh.devices.reshape(2, 4, 4, 4, 2), KA + GA)
    in_specs = (P(KA, None, None, GA), P(None, None, GA), P(KA))
    out_specs = P(GA, KA, None, None, None)
    return jax.shard_map(body, mesh=finer, in_specs=in_specs, out_specs=out_specs, check_vma=False)
```

time: 76.4 us -> 77.3 us (1.012)
  starting transfers between devices: 42.9 us -> 29 us
  blocking collectives: 10.4 us -> 17 us
  Pallas kernels: 12.2 us -> 16.7 us
  waiting for transfers between devices: 6.77 us -> 9.72 us
    ppermute x12, starting transfers between devices: 36.2 us -> 22.2 us  [send(): return lax.ppermute(value, axis, pairs)]
    ppermute x12, waiting for transfers between devices: 2.97 us -> 9.71 us  [send(): return lax.ppermute(value, axis, pairs)]
    all_to_all x1, blocking collectives: 10.4 us -> 17 us  [body(): phi = lax.all_to_all(chosen, XY, 0, 0, tiled=True).reshape(2 * bands, cells)]
    pallas_call x3 -> x4, Pallas kernels: 10.3 us -> 14.8 us  [the longest x1 7.83 us: couple(): pl.pallas_call(kernel, in_specs=[IN_SMEM] + [IN_VMEM] * (2 + parts), out_...]
    all_to_all x1, waiting for transfers between devices: 3.8 us -> 0.01 us  [body(): tagged = lax.all_to_all(tagged, XY, 0, 0, tiled=True)]
  transfers between devices with their start and end apart: 13 -> 13, of which waited for: 3 -> 6; matrix products, arithmetic and copies ran while one was open for 1% -> 1% of each run, Pallas kernels for 5% -> 9%
where the time goes in v4:
time: 77.3 us; the launch traced here: 76.9 us
  starting transfers between devices  29 us (38%)
  blocking collectives  17 us (22%)
  Pallas kernels  16.7 us (22%)
  waiting for transfers between devices  9.72 us (13%)
  local copies, waits for them, and re-layouts  2.77 us (4%)
  other arithmetic  0.99 us (1%)
    ppermute x12, starting transfers between devices, send(): return lax.ppermute(value, axis, pairs)  22.2 us
    all_to_all x1, blocking collectives, body(): phi = lax.all_to_all(chosen, XY, 0, 0, tiled=True).reshape(2 * bands, cells)  17 us
    ppermute x12, waiting for transfers between devices, send(): return lax.ppermute(value, axis, pairs)  9.71 us
    pallas_call x1, Pallas kernels, couple(): pl.pallas_call(kernel, in_specs=[IN_SMEM] + [IN_VMEM] * (2 + parts), out_...  7.83 us
    all_to_all x1, starting transfers between devices, body(): tagged = lax.all_to_all(tagged, XY, 0, 0, tiled=True)  6.75 us
    pallas_call x1, Pallas kernels, choose(): pl.pallas_call(kernel, in_specs=[IN_VMEM, IN_VMEM], out_shape=jax.ShapeDt...  3.79 us
    unnamed x24, local copies, waits for them, and re-layouts  2.77 us
    pallas_call x1, Pallas kernels, pack_lines(): pl.pallas_call(kernel, in_specs=[IN_VMEM, IN_VMEM], out_shape=[jax.ShapeD...  1.87 us
  transfers between devices with their start and end apart: 13, of which 6 were waited for; matrix products, arithmetic and copies ran while one was open for 1% of the time, Pallas kernels for 9%

profile of v4, /device:TPU:1, one launch (start us, length us, event | category | flops | bytes accessed | tf_op | source)
XLA Modules:
  0.0 76.9 jit_solution(3740959429028435243)
XLA Ops:
  0.0 1.9 %shard_map.37 = (bf16[304,256]{1,0:T(8,128)(2,1)}, bf16[304,256]{1,0:T(8,128)(2,1)}, bf16[304,256]{1,0:T(8,128)(2,1)}, bf16[304,256]{1,0:T(8,128)(2,1)}) custom-call(bf16[256,256]{1,0:T(8,128)(2,1)} %bitcast.9, bf16[96,2,256]{2,1,0:T(2,128)(2,1)} %pot_ref.1), custom_call_target="tpu_custom_call" | custom-call | tf_op jit(solution)/shard_map/pallas_call | solution.py:40
  1.9 2.5 %collective-permute-start = (bf16[304,256]{1,0:T(8,128)(2,1)}, bf16[304,256]{1,0:T(8,128)(2,1)S(1)}, u32[]{:S(2)}, u32[]{:S(2)}) collective-permute-start(bf16[304,256]{1,0:T(8,128)(2,1)} %get-tuple-element.10), channel_id=1, source_target_pairs={{0,2},{2,4},{4,6},{6,0},{1,3},{3,5},{5,7},{7,1},{8,10},{10,12},{12... | collective-permute-start | bytes 466952 | tf_op jit(solution)/shard_map/ppermute | solution.py:25
  4.3 2.7 %collective-permute-start.1 = (bf16[304,256]{1,0:T(8,128)(2,1)}, bf16[304,256]{1,0:T(8,128)(2,1)S(1)}, u32[]{:S(2)}, u32[]{:S(2)}) collective-permute-start(bf16[304,256]{1,0:T(8,128)(2,1)} %get-tuple-element.11), channel_id=1, source_target_pairs={{0,6},{2,0},{4,2},{6,4},{1,7},{3,1},{5,3},{7,5},{8,14},{10,8},{12,... | collective-permute-start | bytes 466952 | tf_op jit(solution)/shard_map/ppermute | solution.py:25
  7.0 0.3 collective-permute-start.2
  8.0 1.6 %shard_map.38 = bf16[16,24,256]{2,1,0:T(8,128)(2,1)} custom-call(s32[1]{0:T(128)S(6)} %copy.5.kq_ref, bf16[256,256]{1,0:T(8,128)(2,1)} %bitcast.10), custom_call_target="tpu_custom_call" | custom-call | tf_op jit(solution)/shard_map/pallas_call | solution.py:57
  9.6 6.8 %all-to-all-start = ((bf16[16,24,256]{2,1,0:T(8,128)(2,1)}), bf16[16,24,256]{2,1,0:T(8,128)(2,1)S(1)}, u32[]{:S(2)}, u32[]{:S(2)}) async-start(bf16[16,24,256]{2,1,0:T(8,128)(2,1)} %shard_map.38), calls=%async_computation | async-start | bytes 393216 | tf_op jit(solution)/shard_map/all_to_all | solution.py:184
  16.3 0.0 collective-permute-done
  16.4 5.4 %collective-permute-done.2 = bf16[304,256]{1,0:T(8,128)(2,1)S(1)} collective-permute-done((bf16[304,256]{1,0:T(8,128)(2,1)}, bf16[304,256]{1,0:T(8,128)(2,1)S(1)}, u32[]{:S(2)}, u32[]{:S(2)}) %collective-permute-start.2) | collective-permute-done | bytes 155680 | tf_op jit(solution)/shard_map/ppermute | solution.py:25
  21.7 1.0 %pad_maximum_fusion.lines_ref = bf16[4,304,256]{2,1,0:T(8,128)(2,1)S(1)} fusion(bf16[1,304,256]{2,1,0:T(8,128)(2,1)S(1)} %bitcast.19, bf16[1,304,256]{2,1,0:T(8,128)(2,1)S(1)} %bitcast.18, bf16[1,304,256]{2,1,0:T(8,128)(2,1)S(1)} %bitcast.17, bf16[1,304,256]{2,1,0:T(8,128)(2,1)} %bitcast.16), kind=kLoop, calls=%fused_computation | loop fusion | flops 933888 | bytes 1245184 | tf_op jit(solution)/shard_map/stack | solution.py:188
  22.7 0.6 collective-permute-start.3
  23.3 0.7 copy-done.1
  24.0 1.6 %shard_map.39 = bf16[16,16,256]{2,1,0:T(8,128)(2,1)} custom-call(bf16[16,24,256]{2,1,0:T(8,128)(2,1)} %copy-done.1), custom_call_target="tpu_custom_call" | custom-call | tf_op jit(solution)/shard_map/pallas_call | solution.py:70
  25.6 3.6 %collective-permute-start.4 = (bf16[16,16,256]{2,1,0:T(8,128)(2,1)}, bf16[16,16,256]{2,1,0:T(8,128)(2,1)S(1)}, u32[]{:S(2)}, u32[]{:S(2)}) collective-permute-start(bf16[16,16,256]{2,1,0:T(8,128)(2,1)} %shard_map.39), channel_id=1, source_target_pairs={{0,134},{2,132},{4,130},{6,128},{128,6},{130,4},{132,2},{134,0},{1... | collective-permute-start | bytes 393224 | tf_op jit(solution)/shard_map/ppermute | solution.py:25
  29.2 2.6 %collective-permute-done.4.swapped_ref = bf16[16,16,256]{2,1,0:T(8,128)(2,1)S(1)} collective-permute-done((bf16[16,16,256]{2,1,0:T(8,128)(2,1)}, bf16[16,16,256]{2,1,0:T(8,128)(2,1)S(1)}, u32[]{:S(2)}, u32[]{:S(2)}) %collective-permute-start.4) | collective-permute-done | bytes 131104 | tf_op jit(solution)/shard_map/ppermute | solution.py:25
  31.8 0.6 copy-done.11
  32.4 3.8 %shard_map.40 = bf16[16,16,256]{2,1,0:T(8,128)(2,1)} custom-call(bf16[16,24,256]{2,1,0:T(8,128)(2,1)} %copy-done.1, bf16[16,16,256]{2,1,0:T(8,128)(2,1)} %copy-done.11), custom_call_target="tpu_custom_call" | custom-call | tf_op jit(solution)/shard_map/pallas_call | solution.py:95
  36.2 17.0 %all_to_all.10 = bf16[16,16,256]{2,1,0:T(8,128)(2,1)S(1)} all-to-all(bf16[16,16,256]{2,1,0:T(8,128)(2,1)} %shard_map.40), channel_id=1, replica_groups=mesh['zh'=2,'x'=4,'y'=4,'zl'=4,'c'=2] {'x','y'}, dimensions={0} | all-to-all | bytes 262144 | tf_op jit(solution)/shard_map/all_to_all | solution.py:191
  53.3 1.3 %collective-permute-start.6 = (bf16[256,256]{1,0:T(8,128)(2,1)S(1)}, bf16[256,256]{1,0:T(8,128)(2,1)S(1)}, u32[]{:S(2)}, u32[]{:S(2)}) collective-permute-start(bf16[256,256]{1,0:T(8,128)(2,1)S(1)} %bitcast.12), channel_id=1, source_target_pairs={{0,6},{2,0},{4,2},{6,4},{1,7},{3,1},{5,3},{7,5},{8,14},{10,8},{12,... | collective-permute-start | bytes 393224 | tf_op jit(solution)/shard_map/ppermute | solution.py:25
  54.5 0.3 collective-permute-start.5
  54.8 2.8 %collective-permute-start.8 = (bf16[256,256]{1,0:T(8,128)(2,1)S(1)}, bf16[256,256]{1,0:T(8,128)(2,1)S(1)}, u32[]{:S(2)}, u32[]{:S(2)}) collective-permute-start(bf16[256,256]{1,0:T(8,128)(2,1)S(1)} %bitcast.14), channel_id=1, source_target_pairs={{0,1},{1,0},{2,3},{3,2},{4,5},{5,4},{6,7},{7,6},{8,9},{9,8},{10,11... | collective-permute-start | bytes 393224 | tf_op jit(solution)/shard_map/ppermute | solution.py:25
  57.6 0.7 collective-permute-done.7.refs_3_
  58.4 7.7 %collective-permute-start.11 = (bf16[256,256]{1,0:T(8,128)(2,1)S(1)}, bf16[256,256]{1,0:T(8,128)(2,1)S(1)}, u32[]{:S(2)}, u32[]{:S(2)}) collective-permute-start(bf16[256,256]{1,0:T(8,128)(2,1)S(1)} %collective-permute-done.7.refs_3_), channel_id=1, source_target_pairs={{0,1},{1,0},{2,3},{3,2},{4,5},{5,4},{6,7},{7,6},{8,9},{9,8},{10,11... | collective-permute-start | bytes 393224 | tf_op jit(solution)/shard_map/ppermute | solution.py:25
  66.1 0.1 collective-permute-start.10
  66.2 0.4 collective-permute-start.9
  66.6 0.5 collective-permute-done.11.refs_7_
  67.0 0.4 collective-permute-done.10.refs_6_
  67.4 0.2 collective-permute-done.9.refs_5_
  67.7 0.0 copy-done.8
  67.7 0.4 copy-done.9
  68.1 0.2 copy-done.10
  68.2 0.8 %copy-done.2 = bf16[4,304,256]{2,1,0:T(8,128)(2,1)} copy-done((bf16[4,304,256]{2,1,0:T(8,128)(2,1)}, bf16[4,304,256]{2,1,0:T(8,128)(2,1)S(1)}, u32[]{:S(2)}) %copy-start.2) | copy-done | bytes 622616
  69.1 7.8 %shard_map.41 = f32[12,2,128,128]{3,2,1,0:T(8,128)} custom-call(s32[1]{0:T(128)S(6)} %copy.5.kq_ref, bf16[4,304,256]{2,1,0:T(8,128)(2,1)} %copy-done, bf16[4,304,256]{2,1,0:T(8,128)(2,1)} %copy-done.2, bf16[256,256]{1,0:T(8,128)(2,1)} %bitcast.15, bf16[256,256]{1,0:T(8,128)(2,1)} %copy-done.6, bf16[256,256]{1,0:T(8,128)(2,1)} %copy-done.5, ...), custom_call_target="tpu_custom_call" | custom-call | tf_op jit(solution)/shard_map/pallas_call | solution.py:160
  (25 shorter events, 0.1 us)
Async XLA Ops:
  1.9 14.5 %collective-permute-start = (bf16[304,256]{1,0:T(8,128)(2,1)}, bf16[304,256]{1,0:T(8,128)(2,1)S(1)}, u32[]{:S(2)}, u32[]{:S(2)}) collective-permute-start(bf16[304,256]{1,0:T(8,128)(2,1)} %get-tuple-element.10), channel_id=1, source_target_pairs={{0,2},{2,4},{4,6},{6,0},{1,3},{3,5},{5,7},{7,1},{8,10},{10,12},{12... | collective-permute-start | bytes 466952 | tf_op jit(solution)/shard_map/ppermute | solution.py:25
  4.3 12.0 %collective-permute-start.1 = (bf16[304,256]{1,0:T(8,128)(2,1)}, bf16[304,256]{1,0:T(8,128)(2,1)S(1)}, u32[]{:S(2)}, u32[]{:S(2)}) collective-permute-start(bf16[304,256]{1,0:T(8,128)(2,1)} %get-tuple-element.11), channel_id=1, source_target_pairs={{0,6},{2,0},{4,2},{6,4},{1,7},{3,1},{5,3},{7,5},{8,14},{10,8},{12,... | collective-permute-start | bytes 466952 | tf_op jit(solution)/shard_map/ppermute | solution.py:25
  7.0 14.7 %collective-permute-start.2 = (bf16[304,256]{1,0:T(8,128)(2,1)}, bf16[304,256]{1,0:T(8,128)(2,1)S(1)}, u32[]{:S(2)}, u32[]{:S(2)}) collective-permute-start(bf16[304,256]{1,0:T(8,128)(2,1)} %get-tuple-element.12), channel_id=1, source_target_pairs={{0,4},{2,6},{4,0},{6,2},{1,5},{3,7},{5,1},{7,3},{8,12},{10,14},{12... | collective-permute-start | bytes 466952 | tf_op jit(solution)/shard_map/ppermute | solution.py:25
  9.6 13.8 %all-to-all-start = ((bf16[16,24,256]{2,1,0:T(8,128)(2,1)}), bf16[16,24,256]{2,1,0:T(8,128)(2,1)S(1)}, u32[]{:S(2)}, u32[]{:S(2)}) async-start(bf16[16,24,256]{2,1,0:T(8,128)(2,1)} %shard_map.38), calls=%async_computation | async-start | bytes 393216 | tf_op jit(solution)/shard_map/all_to_all | solution.py:184
  22.7 44.9 %copy-start = (bf16[4,304,256]{2,1,0:T(8,128)(2,1)}, bf16[4,304,256]{2,1,0:T(8,128)(2,1)S(1)}, u32[]{:S(2)}) copy-start(bf16[4,304,256]{2,1,0:T(8,128)(2,1)S(1)} %pad_maximum_fusion.lines_ref) | copy-start | bytes 1867780
  22.7 44.9 %collective-permute-start.3 = (bf16[4,304,256]{2,1,0:T(8,128)(2,1)S(1)}, bf16[4,304,256]{2,1,0:T(8,128)(2,1)S(1)}, u32[]{:S(2)}, u32[]{:S(2)}) collective-permute-start(bf16[4,304,256]{2,1,0:T(8,128)(2,1)S(1)} %pad_maximum_fusion.lines_ref), channel_id=1, source_target_pairs={{0,1},{1,0},{2,3},{3,2},{4,5},{5,4},{6,7},{7,6},{8,9},{9,8},{10,11... | collective-permute-start | bytes 1867784 | tf_op jit(solution)/shard_map/ppermute | solution.py:25
  23.3 0.7 copy-start.1
  25.6 6.2 %collective-permute-start.4 = (bf16[16,16,256]{2,1,0:T(8,128)(2,1)}, bf16[16,16,256]{2,1,0:T(8,128)(2,1)S(1)}, u32[]{:S(2)}, u32[]{:S(2)}) collective-permute-start(bf16[16,16,256]{2,1,0:T(8,128)(2,1)} %shard_map.39), channel_id=1, source_target_pairs={{0,134},{2,132},{4,130},{6,128},{128,6},{130,4},{132,2},{134,0},{1... | collective-permute-start | bytes 393224 | tf_op jit(solution)/shard_map/ppermute | solution.py:25
  31.8 0.7 copy-start.11
  53.3 14.3 %copy-start.3 = (bf16[16,16,256]{2,1,0:T(8,128)(2,1)}, bf16[16,16,256]{2,1,0:T(8,128)(2,1)S(1)}, u32[]{:S(2)}) copy-start(bf16[16,16,256]{2,1,0:T(8,128)(2,1)S(1)} %all_to_all.10) | copy-start | bytes 393220
  53.3 5.1 %collective-permute-start.7 = (bf16[256,256]{1,0:T(8,128)(2,1)S(1)}, bf16[256,256]{1,0:T(8,128)(2,1)S(1)}, u32[]{:S(2)}, u32[]{:S(2)}) collective-permute-start(bf16[256,256]{1,0:T(8,128)(2,1)S(1)} %bitcast.11), channel_id=1, source_target_pairs={{0,4},{2,6},{4,0},{6,2},{1,5},{3,7},{5,1},{7,3},{8,12},{10,14},{12... | collective-permute-start | bytes 393224 | tf_op jit(solution)/shard_map/ppermute | solution.py:25
  53.3 12.8 %collective-permute-start.6 = (bf16[256,256]{1,0:T(8,128)(2,1)S(1)}, bf16[256,256]{1,0:T(8,128)(2,1)S(1)}, u32[]{:S(2)}, u32[]{:S(2)}) collective-permute-start(bf16[256,256]{1,0:T(8,128)(2,1)S(1)} %bitcast.12), channel_id=1, source_target_pairs={{0,6},{2,0},{4,2},{6,4},{1,7},{3,1},{5,3},{7,5},{8,14},{10,8},{12,... | collective-permute-start | bytes 393224 | tf_op jit(solution)/shard_map/ppermute | solution.py:25
  54.5 11.6 %collective-permute-start.5 = (bf16[256,256]{1,0:T(8,128)(2,1)S(1)}, bf16[256,256]{1,0:T(8,128)(2,1)S(1)}, u32[]{:S(2)}, u32[]{:S(2)}) collective-permute-start(bf16[256,256]{1,0:T(8,128)(2,1)S(1)} %bitcast.13), channel_id=1, source_target_pairs={{0,2},{2,4},{4,6},{6,0},{1,3},{3,5},{5,7},{7,1},{8,10},{10,12},{12... | collective-permute-start | bytes 393224 | tf_op jit(solution)/shard_map/ppermute | solution.py:25
  54.8 11.8 %collective-permute-start.8 = (bf16[256,256]{1,0:T(8,128)(2,1)S(1)}, bf16[256,256]{1,0:T(8,128)(2,1)S(1)}, u32[]{:S(2)}, u32[]{:S(2)}) collective-permute-start(bf16[256,256]{1,0:T(8,128)(2,1)S(1)} %bitcast.14), channel_id=1, source_target_pairs={{0,1},{1,0},{2,3},{3,2},{4,5},{5,4},{6,7},{7,6},{8,9},{9,8},{10,11... | collective-permute-start | bytes 393224 | tf_op jit(solution)/shard_map/ppermute | solution.py:25
  58.4 9.2 %copy-start.4 = (bf16[256,256]{1,0:T(8,128)(2,1)}, bf16[256,256]{1,0:T(8,128)(2,1)S(1)}, u32[]{:S(2)}) copy-start(bf16[256,256]{1,0:T(8,128)(2,1)S(1)} %collective-permute-done.7.refs_3_) | copy-start | bytes 393220
  58.4 8.6 %collective-permute-start.11 = (bf16[256,256]{1,0:T(8,128)(2,1)S(1)}, bf16[256,256]{1,0:T(8,128)(2,1)S(1)}, u32[]{:S(2)}, u32[]{:S(2)}) collective-permute-start(bf16[256,256]{1,0:T(8,128)(2,1)S(1)} %collective-permute-done.7.refs_3_), channel_id=1, source_target_pairs={{0,1},{1,0},{2,3},{3,2},{4,5},{5,4},{6,7},{7,6},{8,9},{9,8},{10,11... | collective-permute-start | bytes 393224 | tf_op jit(solution)/shard_map/ppermute | solution.py:25
  66.1 1.6 %copy-start.5 = (bf16[256,256]{1,0:T(8,128)(2,1)}, bf16[256,256]{1,0:T(8,128)(2,1)S(1)}, u32[]{:S(2)}) copy-start(bf16[256,256]{1,0:T(8,128)(2,1)S(1)} %collective-permute-done.6.refs_2_) | copy-start | bytes 393220
  66.1 1.3 %collective-permute-start.10 = (bf16[256,256]{1,0:T(8,128)(2,1)S(1)}, bf16[256,256]{1,0:T(8,128)(2,1)S(1)}, u32[]{:S(2)}, u32[]{:S(2)}) collective-permute-start(bf16[256,256]{1,0:T(8,128)(2,1)S(1)} %collective-permute-done.6.refs_2_), channel_id=1, source_target_pairs={{0,1},{1,0},{2,3},{3,2},{4,5},{5,4},{6,7},{7,6},{8,9},{9,8},{10,11... | collective-permute-start | bytes 393224 | tf_op jit(solution)/shard_map/ppermute | solution.py:25
  66.2 1.5 %copy-start.6 = (bf16[256,256]{1,0:T(8,128)(2,1)}, bf16[256,256]{1,0:T(8,128)(2,1)S(1)}, u32[]{:S(2)}) copy-start(bf16[256,256]{1,0:T(8,128)(2,1)S(1)} %collective-permute-done.5.refs_1_) | copy-start | bytes 393220
  66.2 1.4 %collective-permute-start.9 = (bf16[256,256]{1,0:T(8,128)(2,1)S(1)}, bf16[256,256]{1,0:T(8,128)(2,1)S(1)}, u32[]{:S(2)}, u32[]{:S(2)}) collective-permute-start(bf16[256,256]{1,0:T(8,128)(2,1)S(1)} %collective-permute-done.5.refs_1_), channel_id=1, source_target_pairs={{0,1},{1,0},{2,3},{3,2},{4,5},{5,4},{6,7},{7,6},{8,9},{9,8},{10,11... | collective-permute-start | bytes 393224 | tf_op jit(solution)/shard_map/ppermute | solution.py:25
  66.6 1.1 %copy-start.7 = (bf16[256,256]{1,0:T(8,128)(2,1)}, bf16[256,256]{1,0:T(8,128)(2,1)S(1)}, u32[]{:S(2)}) copy-start(bf16[256,256]{1,0:T(8,128)(2,1)S(1)} %collective-permute-done.8.refs_4_) | copy-start | bytes 393220
  67.0 0.6 copy-start.8
  67.4 0.7 copy-start.9
  67.6 0.6 copy-start.10
  68.2 0.8 %copy-start.2 = (bf16[4,304,256]{2,1,0:T(8,128)(2,1)}, bf16[4,304,256]{2,1,0:T(8,128)(2,1)S(1)}, u32[]{:S(2)}) copy-start(bf16[4,304,256]{2,1,0:T(8,128)(2,1)S(1)} %collective-permute-done.3.twins_ref) | copy-start | bytes 1867780

commit v5 on v4

--- a/solution.py
+++ b/solution.py
@@ -13,16 +13,13 @@
 MIRROR = [(z, 7 - z) for z in range(8)]
 STEPS = (0, 1, 3, 2)
 TAG = 8
+VMEM_LIMIT = 20 * 2**20
 IN_SMEM = pl.BlockSpec(memory_space=pltpu.SMEM)
 IN_VMEM = pl.BlockSpec(memory_space=pltpu.VMEM)
 
 
 def ring(step, size=4):
     return [(i, (i + step) % size) for i in range(size)]
-
-
-def send(value, axis, pairs):
-    return lax.ppermute(value, axis, pairs)
 
 
 def pack_lines(slab, potential):
@@ -44,59 +41,40 @@
     )(slab, potential)
 
 
-def pack_spread(slab, kq):
+def pack_spread(slab, swapped, kq):
     rows, cells = slab.shape
     piece = rows // 16
 
-    def kernel(kq_ref, slab_ref, out):
+    def kernel(kq_ref, slab_ref, swapped_ref, out):
         tag = jnp.full((TAG, cells), kq_ref[0].astype(jnp.float32)).astype(slab.dtype)
         for j in range(16):
             out[j, :piece] = slab_ref[j * piece : (j + 1) * piece]
-            out[j, piece:] = tag
+            out[j, piece : 2 * piece] = swapped_ref[j * piece : (j + 1) * piece]
+            out[j, 2 * piece :] = tag
 
     return pl.pallas_call(
         kernel,
-        in_specs=[IN_SMEM, IN_VMEM],
-        out_shape=jax.ShapeDtypeStruct((16, piece + TAG, cells), slab.dtype),
-    )(kq, slab)
+        in_specs=[IN_SMEM, IN_VMEM, IN_VMEM],
+        out_shape=jax.ShapeDtypeStruct((16, 2 * piece + TAG, cells), slab.dtype),
+    )(kq, slab, swapped)
 
 
-def strip(tagged):
-    count, rows, cells = tagged.shape
+def choose(pieces):
+    count, rows, cells = pieces.shape
+    piece = (rows - TAG) // 2
 
     def kernel(ref, out):
-        out[...] = ref[:, : rows - TAG]
+        zh = lax.axis_index("zh")
+        for d in range(count):
+            source = jnp.max(ref[d, 2 * piece :, :128].astype(jnp.float32)).astype(jnp.int32)
+            side = jnp.where(source // count == zh, 0, piece)
+            out[d] = ref[lax.rem(source, count), pl.ds(pl.multiple_of(side, piece), piece), :]
 
     return pl.pallas_call(
         kernel,
         in_specs=[IN_VMEM],
-        out_shape=jax.ShapeDtypeStruct((count, rows - TAG, cells), tagged.dtype),
-    )(tagged)
-
-
-def choose(tagged, swapped):
-    count, piece, _ = swapped.shape
-
-    def kernel(ref, swapped_ref, out):
-        zh = lax.axis_index("zh")
-        for d in range(count):
-            source = jnp.max(ref[d, piece:, :128].astype(jnp.float32)).astype(jnp.int32)
-            block = lax.rem(source, count)
-            here = source // count == zh
-
-            @pl.when(here)
-            def _():
-                out[d] = ref[block, :piece]
-
-            @pl.when(jnp.logical_not(here))
-            def _():
-                out[d] = swapped_ref[block]
-
-    return pl.pallas_call(
-        kernel,
-        in_specs=[IN_VMEM, IN_VMEM],
-        out_shape=jax.ShapeDtypeStruct(swapped.shape, swapped.dtype),
-    )(tagged, swapped)
+        out_shape=jax.ShapeDtypeStruct((count, piece, cells), pieces.dtype),
+    )(pieces)
 
 
 def couple(kq, lines, twins, others, bands, modes):
@@ -172,6 +150,7 @@
             pltpu.VMEM((modes, 2, bands, bands), jnp.float32),
             pltpu.SemaphoreType.DMA((modes // 2,)),
         ],
+        compiler_params=pltpu.CompilerParams(vmem_limit_bytes=VMEM_LIMIT),
     )(kq, lines, twins, *others)
 
 
@@ -180,18 +159,18 @@
     modes = dvscf.shape[0] // 8
     slab = psi.reshape(2 * bands, cells)
 
-    tagged = pack_spread(slab, kq_map)
-    tagged = lax.all_to_all(tagged, XY, 0, 0, tiled=True)
-    swapped = send(strip(tagged), ("zh", "zl"), MIRROR)
+    swapped = lax.ppermute(slab, ("zh", "zl"), MIRROR)
     packs = pack_lines(slab, dvscf)
-    lines = [packs[0]] + [send(packs[i], "zl", ring(STEPS[i])) for i in (1, 2, 3)]
+    lines = [packs[0]] + [lax.ppermute(packs[i], "zl", ring(STEPS[i])) for i in (1, 2, 3)]
     lines = jnp.stack(lines)
-    twins = send(lines, "c", SWAP)
-    chosen = choose(tagged, swapped)
-    phi = lax.all_to_all(chosen, XY, 0, 0, tiled=True).reshape(2 * bands, cells)
+    twins = lax.ppermute(lines, "c", SWAP)
 
-    others = [phi] + [send(phi, "zl", ring(STEPS[i])) for i in (1, 2, 3)]
-    others += [send(o, "c", SWAP) for o in others]
+    pieces = pack_spread(slab, swapped, kq_map)
+    pieces = lax.all_to_all(pieces, XY, 0, 0, tiled=True)
+    phi = lax.all_to_all(choose(pieces), XY, 0, 0, tiled=True).reshape(2 * bands, cells)
+
+    others = [phi] + [lax.ppermute(phi, "zl", ring(STEPS[i])) for i in (1, 2, 3)]
+    others += [lax.ppermute(o, "c", SWAP) for o in others]
     out = couple(kq_map, lines, twins, others, bands, modes)
     return out[:, None]
 

time: 77.3 us -> 75.2 us (0.973)
  starting transfers between devices: 29 us -> 42.9 us
  blocking collectives: 17 us -> 10.4 us
  Pallas kernels: 16.7 us -> 11.7 us
  waiting for transfers between devices: 9.72 us -> 6.82 us
  local copies, waits for them, and re-layouts: 2.77 us -> 1.38 us
    ppermute x12, starting transfers between devices: 22.2 us -> 36.2 us  [the longest x3 13.8 us: body(): lax.ppermute(phi, 'zl', ring(STEPS[i]))]
    ppermute x12, waiting for transfers between devices: 9.71 us -> 3.01 us  [the longest x1 2.02 us: body(): swapped = lax.ppermute(slab, ('zh', 'zl'), MIRROR)]
    all_to_all x1, blocking collectives: 17 us -> 10.4 us  [body(): lax.all_to_all(choose(pieces), XY, 0, 0, tiled=True)]
    all_to_all x1, waiting for transfers between devices: 0.01 us -> 3.81 us  [body(): pieces = lax.all_to_all(pieces, XY, 0, 0, tiled=True)]
    pallas_call x3 -> x2, Pallas kernels: 6.97 us -> 3.59 us  [the longest x1 1.88 us: choose(): pl.pallas_call(kernel, in_specs=[IN_VMEM], out_shape=jax.ShapeDtypeStruct...]
    pallas_call x1, Pallas kernels: 7.83 us -> 6.29 us  [couple(): pl.pallas_call(kernel, in_specs=[IN_SMEM] + [IN_VMEM] * (2 + parts), out_...]
    unnamed x24 -> x4, local copies, waits for them, and re-layouts: 2.77 us -> 1.38 us
  transfers between devices with their start and end apart: 13 -> 13, of which waited for: 6 -> 3; matrix products, arithmetic and copies ran while one was open for 1% -> 1% of each run, Pallas kernels for 9% -> 5%
where the time goes in v5:
time: 75.2 us; the launch traced here: 74.9 us
  starting transfers between devices  42.9 us (57%)
  Pallas kernels  11.7 us (16%)
  blocking collectives  10.4 us (14%)
  waiting for transfers between devices  6.82 us (9%)
  local copies, waits for them, and re-layouts  1.38 us (2%)
  other arithmetic  0.99 us (1%)
    ppermute x3, starting transfers between devices, body(): lax.ppermute(phi, 'zl', ring(STEPS[i]))  13.8 us
    ppermute x4, starting transfers between devices, body(): others += [lax.ppermute(o, 'c', SWAP) for o in others]  10.6 us
    all_to_all x1, blocking collectives, body(): lax.all_to_all(choose(pieces), XY, 0, 0, tiled=True)  10.4 us
    all_to_all x1, starting transfers between devices, body(): pieces = lax.all_to_all(pieces, XY, 0, 0, tiled=True)  6.64 us
    pallas_call x1, Pallas kernels, couple(): pl.pallas_call(kernel, in_specs=[IN_SMEM] + [IN_VMEM] * (2 + parts), out_...  6.29 us
    ppermute x3, starting transfers between devices, body(): lax.ppermute(packs[i], 'zl', ring(STEPS[i]))  5.45 us
    all_to_all x1, waiting for transfers between devices, body(): pieces = lax.all_to_all(pieces, XY, 0, 0, tiled=True)  3.81 us
    ppermute x1, starting transfers between devices, body(): swapped = lax.ppermute(slab, ('zh', 'zl'), MIRROR)  3.58 us
  transfers between devices with their start and end apart: 13, of which 3 were waited for; matrix products, arithmetic and copies ran while one was open for 1% of the time, Pallas kernels for 5%

profile of v5, /device:TPU:1, one launch (start us, length us, event | category | flops | bytes accessed | tf_op | source)
XLA Modules:
  0.0 74.9 jit_solution(17724921760192069592)
XLA Ops:
  0.0 1.8 %shard_map.37 = (bf16[304,256]{1,0:T(8,128)(2,1)}, bf16[304,256]{1,0:T(8,128)(2,1)}, bf16[304,256]{1,0:T(8,128)(2,1)}, bf16[304,256]{1,0:T(8,128)(2,1)}) custom-call(bf16[256,256]{1,0:T(8,128)(2,1)} %bitcast.14, bf16[96,2,256]{2,1,0:T(2,128)(2,1)} %pot_ref.1), custom_call_target="tpu_custom_call" | custom-call | tf_op jit(solution)/shard_map/pallas_call | solution.py:37
  1.8 2.5 %collective-permute-start = (bf16[304,256]{1,0:T(8,128)(2,1)}, bf16[304,256]{1,0:T(8,128)(2,1)S(1)}, u32[]{:S(2)}, u32[]{:S(2)}) collective-permute-start(bf16[304,256]{1,0:T(8,128)(2,1)} %get-tuple-element.10), channel_id=1, source_target_pairs={{0,2},{2,4},{4,6},{6,0},{1,3},{3,5},{5,7},{7,1},{8,10},{10,12},{12... | collective-permute-start | bytes 466952 | tf_op jit(solution)/shard_map/ppermute | solution.py:164
  4.3 2.7 %collective-permute-start.1 = (bf16[304,256]{1,0:T(8,128)(2,1)}, bf16[304,256]{1,0:T(8,128)(2,1)S(1)}, u32[]{:S(2)}, u32[]{:S(2)}) collective-permute-start(bf16[304,256]{1,0:T(8,128)(2,1)} %get-tuple-element.11), channel_id=1, source_target_pairs={{0,6},{2,0},{4,2},{6,4},{1,7},{3,1},{5,3},{7,5},{8,14},{10,8},{12,... | collective-permute-start | bytes 466952 | tf_op jit(solution)/shard_map/ppermute | solution.py:164
  7.0 0.3 collective-permute-start.2
  7.3 3.6 %collective-permute-start.4 = (bf16[256,256]{1,0:T(8,128)(2,1)}, bf16[256,256]{1,0:T(8,128)(2,1)S(1)}, u32[]{:S(2)}, u32[]{:S(2)}) collective-permute-start(bf16[256,256]{1,0:T(8,128)(2,1)} %bitcast.15), channel_id=1, source_target_pairs={{0,134},{2,132},{4,130},{6,128},{128,6},{130,4},{132,2},{134,0},{1... | collective-permute-start | bytes 393224 | tf_op jit(solution)/shard_map/ppermute | solution.py:162
  11.5 2.0 %collective-permute-done.4.swapped_ref = bf16[256,256]{1,0:T(8,128)(2,1)S(1)} collective-permute-done((bf16[256,256]{1,0:T(8,128)(2,1)}, bf16[256,256]{1,0:T(8,128)(2,1)S(1)}, u32[]{:S(2)}, u32[]{:S(2)}) %collective-permute-start.4) | collective-permute-done | bytes 131104 | tf_op jit(solution)/shard_map/ppermute | solution.py:162
  13.6 0.7 copy-done.1
  14.2 1.7 %shard_map.38 = bf16[16,40,256]{2,1,0:T(8,128)(2,1)} custom-call(s32[1]{0:T(128)S(6)} %copy.5.kq_ref, bf16[256,256]{1,0:T(8,128)(2,1)} %bitcast.16, bf16[256,256]{1,0:T(8,128)(2,1)} %copy-done.1), custom_call_target="tpu_custom_call" | custom-call | tf_op jit(solution)/shard_map/pallas_call | solution.py:55
  15.9 6.6 %all-to-all-start = ((bf16[16,40,256]{2,1,0:T(8,128)(2,1)}), bf16[16,40,256]{2,1,0:T(8,128)(2,1)S(1)}, u32[]{:S(2)}, u32[]{:S(2)}) async-start(bf16[16,40,256]{2,1,0:T(8,128)(2,1)} %shard_map.38), calls=%async_computation | async-start | bytes 655360 | tf_op jit(solution)/shard_map/all_to_all | solution.py:169
  22.6 0.0 collective-permute-done
  22.6 0.0 collective-permute-done.1
  22.6 0.0 collective-permute-done.2
  22.6 1.0 %pad_maximum_fusion.lines_ref = bf16[4,304,256]{2,1,0:T(8,128)(2,1)S(1)} fusion(bf16[1,304,256]{2,1,0:T(8,128)(2,1)S(1)} %bitcast.20, bf16[1,304,256]{2,1,0:T(8,128)(2,1)S(1)} %bitcast.19, bf16[1,304,256]{2,1,0:T(8,128)(2,1)S(1)} %bitcast.18, bf16[1,304,256]{2,1,0:T(8,128)(2,1)} %bitcast.17), kind=kLoop, calls=%fused_computation | loop fusion | flops 933888 | bytes 1245184 | tf_op jit(solution)/shard_map/stack | solution.py:165
  23.6 2.9 %collective-permute-start.3 = (bf16[4,304,256]{2,1,0:T(8,128)(2,1)S(1)}, bf16[4,304,256]{2,1,0:T(8,128)(2,1)S(1)}, u32[]{:S(2)}, u32[]{:S(2)}) collective-permute-start(bf16[4,304,256]{2,1,0:T(8,128)(2,1)S(1)} %pad_maximum_fusion.lines_ref), channel_id=1, source_target_pairs={{0,1},{1,0},{2,3},{3,2},{4,5},{5,4},{6,7},{7,6},{8,9},{9,8},{10,11... | collective-permute-start | bytes 1867784 | tf_op jit(solution)/shard_map/ppermute | solution.py:166
  26.5 3.8 %all-to-all-done.ref = bf16[16,40,256]{2,1,0:T(8,128)(2,1)S(1)} async-done(((bf16[16,40,256]{2,1,0:T(8,128)(2,1)}), bf16[16,40,256]{2,1,0:T(8,128)(2,1)S(1)}, u32[]{:S(2)}, u32[]{:S(2)}) %all-to-all-start) | async-done | bytes 327712 | tf_op jit(solution)/shard_map/all_to_all | solution.py:169
  30.3 0.7 copy-done
  31.0 1.9 %shard_map.39 = bf16[16,16,256]{2,1,0:T(8,128)(2,1)} custom-call(bf16[16,40,256]{2,1,0:T(8,128)(2,1)} %copy-done), custom_call_target="tpu_custom_call" | custom-call | tf_op jit(solution)/shard_map/pallas_call | solution.py:73
  32.9 10.4 %all_to_all.10 = bf16[16,16,256]{2,1,0:T(8,128)(2,1)S(1)} all-to-all(bf16[16,16,256]{2,1,0:T(8,128)(2,1)} %shard_map.39), channel_id=1, replica_groups=mesh['zh'=2,'x'=4,'y'=4,'zl'=4,'c'=2] {'x','y'}, dimensions={0} | all-to-all | bytes 262144 | tf_op jit(solution)/shard_map/all_to_all | solution.py:170
  43.2 11.2 %collective-permute-start.7 = (bf16[256,256]{1,0:T(8,128)(2,1)S(1)}, bf16[256,256]{1,0:T(8,128)(2,1)S(1)}, u32[]{:S(2)}, u32[]{:S(2)}) collective-permute-start(bf16[256,256]{1,0:T(8,128)(2,1)S(1)} %bitcast.9), channel_id=1, source_target_pairs={{0,4},{2,6},{4,0},{6,2},{1,5},{3,7},{5,1},{7,3},{8,12},{10,14},{12... | collective-permute-start | bytes 393224 | tf_op jit(solution)/shard_map/ppermute | solution.py:172
  54.5 2.5 %collective-permute-start.6 = (bf16[256,256]{1,0:T(8,128)(2,1)S(1)}, bf16[256,256]{1,0:T(8,128)(2,1)S(1)}, u32[]{:S(2)}, u32[]{:S(2)}) collective-permute-start(bf16[256,256]{1,0:T(8,128)(2,1)S(1)} %bitcast.10), channel_id=1, source_target_pairs={{0,6},{2,0},{4,2},{6,4},{1,7},{3,1},{5,3},{7,5},{8,14},{10,8},{12,... | collective-permute-start | bytes 393224 | tf_op jit(solution)/shard_map/ppermute | solution.py:172
  57.0 0.0 collective-permute-start.5
  57.0 3.9 %collective-permute-start.8 = (bf16[256,256]{1,0:T(8,128)(2,1)S(1)}, bf16[256,256]{1,0:T(8,128)(2,1)S(1)}, u32[]{:S(2)}, u32[]{:S(2)}) collective-permute-start(bf16[256,256]{1,0:T(8,128)(2,1)S(1)} %bitcast.12), channel_id=1, source_target_pairs={{0,1},{1,0},{2,3},{3,2},{4,5},{5,4},{6,7},{7,6},{8,9},{9,8},{10,11... | collective-permute-start | bytes 393224 | tf_op jit(solution)/shard_map/ppermute | solution.py:173
  60.9 0.0 collective-permute-done.7.refs_3_
  60.9 1.3 %collective-permute-start.11 = (bf16[256,256]{1,0:T(8,128)(2,1)S(1)}, bf16[256,256]{1,0:T(8,128)(2,1)S(1)}, u32[]{:S(2)}, u32[]{:S(2)}) collective-permute-start(bf16[256,256]{1,0:T(8,128)(2,1)S(1)} %collective-permute-done.7.refs_3_), channel_id=1, source_target_pairs={{0,1},{1,0},{2,3},{3,2},{4,5},{5,4},{6,7},{7,6},{8,9},{9,8},{10,11... | collective-permute-start | bytes 393224 | tf_op jit(solution)/shard_map/ppermute | solution.py:173
  62.2 2.7 %collective-permute-start.10 = (bf16[256,256]{1,0:T(8,128)(2,1)S(1)}, bf16[256,256]{1,0:T(8,128)(2,1)S(1)}, u32[]{:S(2)}, u32[]{:S(2)}) collective-permute-start(bf16[256,256]{1,0:T(8,128)(2,1)S(1)} %collective-permute-done.6.refs_2_), channel_id=1, source_target_pairs={{0,1},{1,0},{2,3},{3,2},{4,5},{5,4},{6,7},{7,6},{8,9},{9,8},{10,11... | collective-permute-start | bytes 393224 | tf_op jit(solution)/shard_map/ppermute | solution.py:173
  64.9 0.0 collective-permute-done.5.refs_1_
  64.9 2.7 %collective-permute-start.9 = (bf16[256,256]{1,0:T(8,128)(2,1)S(1)}, bf16[256,256]{1,0:T(8,128)(2,1)S(1)}, u32[]{:S(2)}, u32[]{:S(2)}) collective-permute-start(bf16[256,256]{1,0:T(8,128)(2,1)S(1)} %collective-permute-done.5.refs_1_), channel_id=1, source_target_pairs={{0,1},{1,0},{2,3},{3,2},{4,5},{5,4},{6,7},{7,6},{8,9},{9,8},{10,11... | collective-permute-start | bytes 393224 | tf_op jit(solution)/shard_map/ppermute | solution.py:173
  67.6 0.0 collective-permute-done.8.refs_4_
  67.6 0.0 collective-permute-done.3.twins_ref
  67.6 0.0 collective-permute-done.10.refs_6_
  67.6 1.0 %collective-permute-done.9.refs_5_ = bf16[256,256]{1,0:T(8,128)(2,1)S(1)} collective-permute-done((bf16[256,256]{1,0:T(8,128)(2,1)S(1)}, bf16[256,256]{1,0:T(8,128)(2,1)S(1)}, u32[]{:S(2)}, u32[]{:S(2)}) %collective-permute-start.9) | collective-permute-done | bytes 131104 | tf_op jit(solution)/shard_map/ppermute | solution.py:173
  68.6 6.3 %shard_map.40 = f32[12,2,128,128]{3,2,1,0:T(8,128)} custom-call(s32[1]{0:T(128)S(6)} %copy.5.kq_ref, bf16[4,304,256]{2,1,0:T(8,128)(2,1)S(1)} %pad_maximum_fusion.lines_ref, bf16[4,304,256]{2,1,0:T(8,128)(2,1)S(1)} %collective-permute-done.3.twins_ref, bf16[256,256]{1,0:T(8,128)(2,1)S(1)} %bitcast.13, bf16[256,256]{1,0:T(8,128)(2,1)S(1)} %collective-permute-done.5.refs_1_, ...), custom_call_target="tpu_custom_call" | custom-call | tf_op jit(solution)/shard_map/pallas_call | solution.py:138
  (4 shorter events, 0.0 us)
Async XLA Ops:
  1.8 20.7 %collective-permute-start = (bf16[304,256]{1,0:T(8,128)(2,1)}, bf16[304,256]{1,0:T(8,128)(2,1)S(1)}, u32[]{:S(2)}, u32[]{:S(2)}) collective-permute-start(bf16[304,256]{1,0:T(8,128)(2,1)} %get-tuple-element.10), channel_id=1, source_target_pairs={{0,2},{2,4},{4,6},{6,0},{1,3},{3,5},{5,7},{7,1},{8,10},{10,12},{12... | collective-permute-start | bytes 466952 | tf_op jit(solution)/shard_map/ppermute | solution.py:164
  4.3 18.3 %collective-permute-start.1 = (bf16[304,256]{1,0:T(8,128)(2,1)}, bf16[304,256]{1,0:T(8,128)(2,1)S(1)}, u32[]{:S(2)}, u32[]{:S(2)}) collective-permute-start(bf16[304,256]{1,0:T(8,128)(2,1)} %get-tuple-element.11), channel_id=1, source_target_pairs={{0,6},{2,0},{4,2},{6,4},{1,7},{3,1},{5,3},{7,5},{8,14},{10,8},{12,... | collective-permute-start | bytes 466952 | tf_op jit(solution)/shard_map/ppermute | solution.py:164
  7.0 15.6 %collective-permute-start.2 = (bf16[304,256]{1,0:T(8,128)(2,1)}, bf16[304,256]{1,0:T(8,128)(2,1)S(1)}, u32[]{:S(2)}, u32[]{:S(2)}) collective-permute-start(bf16[304,256]{1,0:T(8,128)(2,1)} %get-tuple-element.12), channel_id=1, source_target_pairs={{0,4},{2,6},{4,0},{6,2},{1,5},{3,7},{5,1},{7,3},{8,12},{10,14},{12... | collective-permute-start | bytes 466952 | tf_op jit(solution)/shard_map/ppermute | solution.py:164
  7.3 6.3 %collective-permute-start.4 = (bf16[256,256]{1,0:T(8,128)(2,1)}, bf16[256,256]{1,0:T(8,128)(2,1)S(1)}, u32[]{:S(2)}, u32[]{:S(2)}) collective-permute-start(bf16[256,256]{1,0:T(8,128)(2,1)} %bitcast.15), channel_id=1, source_target_pairs={{0,134},{2,132},{4,130},{6,128},{128,6},{130,4},{132,2},{134,0},{1... | collective-permute-start | bytes 393224 | tf_op jit(solution)/shard_map/ppermute | solution.py:162
  13.6 0.7 copy-start.1
  15.9 14.3 %all-to-all-start = ((bf16[16,40,256]{2,1,0:T(8,128)(2,1)}), bf16[16,40,256]{2,1,0:T(8,128)(2,1)S(1)}, u32[]{:S(2)}, u32[]{:S(2)}) async-start(bf16[16,40,256]{2,1,0:T(8,128)(2,1)} %shard_map.38), calls=%async_computation | async-start | bytes 655360 | tf_op jit(solution)/shard_map/all_to_all | solution.py:169
  23.6 44.0 %collective-permute-start.3 = (bf16[4,304,256]{2,1,0:T(8,128)(2,1)S(1)}, bf16[4,304,256]{2,1,0:T(8,128)(2,1)S(1)}, u32[]{:S(2)}, u32[]{:S(2)}) collective-permute-start(bf16[4,304,256]{2,1,0:T(8,128)(2,1)S(1)} %pad_maximum_fusion.lines_ref), channel_id=1, source_target_pairs={{0,1},{1,0},{2,3},{3,2},{4,5},{5,4},{6,7},{7,6},{8,9},{9,8},{10,11... | collective-permute-start | bytes 1867784 | tf_op jit(solution)/shard_map/ppermute | solution.py:166
  30.3 0.7 copy-start
  43.2 17.7 %collective-permute-start.7 = (bf16[256,256]{1,0:T(8,128)(2,1)S(1)}, bf16[256,256]{1,0:T(8,128)(2,1)S(1)}, u32[]{:S(2)}, u32[]{:S(2)}) collective-permute-start(bf16[256,256]{1,0:T(8,128)(2,1)S(1)} %bitcast.9), channel_id=1, source_target_pairs={{0,4},{2,6},{4,0},{6,2},{1,5},{3,7},{5,1},{7,3},{8,12},{10,14},{12... | collective-permute-start | bytes 393224 | tf_op jit(solution)/shard_map/ppermute | solution.py:172
  54.5 7.7 %collective-permute-start.6 = (bf16[256,256]{1,0:T(8,128)(2,1)S(1)}, bf16[256,256]{1,0:T(8,128)(2,1)S(1)}, u32[]{:S(2)}, u32[]{:S(2)}) collective-permute-start(bf16[256,256]{1,0:T(8,128)(2,1)S(1)} %bitcast.10), channel_id=1, source_target_pairs={{0,6},{2,0},{4,2},{6,4},{1,7},{3,1},{5,3},{7,5},{8,14},{10,8},{12,... | collective-permute-start | bytes 393224 | tf_op jit(solution)/shard_map/ppermute | solution.py:172
  57.0 7.9 %collective-permute-start.5 = (bf16[256,256]{1,0:T(8,128)(2,1)S(1)}, bf16[256,256]{1,0:T(8,128)(2,1)S(1)}, u32[]{:S(2)}, u32[]{:S(2)}) collective-permute-start(bf16[256,256]{1,0:T(8,128)(2,1)S(1)} %bitcast.11), channel_id=1, source_target_pairs={{0,2},{2,4},{4,6},{6,0},{1,3},{3,5},{5,7},{7,1},{8,10},{10,12},{12... | collective-permute-start | bytes 393224 | tf_op jit(solution)/shard_map/ppermute | solution.py:172
  57.0 10.6 %collective-permute-start.8 = (bf16[256,256]{1,0:T(8,128)(2,1)S(1)}, bf16[256,256]{1,0:T(8,128)(2,1)S(1)}, u32[]{:S(2)}, u32[]{:S(2)}) collective-permute-start(bf16[256,256]{1,0:T(8,128)(2,1)S(1)} %bitcast.12), channel_id=1, source_target_pairs={{0,1},{1,0},{2,3},{3,2},{4,5},{5,4},{6,7},{7,6},{8,9},{9,8},{10,11... | collective-permute-start | bytes 393224 | tf_op jit(solution)/shard_map/ppermute | solution.py:173
  60.9 6.7 %collective-permute-start.11 = (bf16[256,256]{1,0:T(8,128)(2,1)S(1)}, bf16[256,256]{1,0:T(8,128)(2,1)S(1)}, u32[]{:S(2)}, u32[]{:S(2)}) collective-permute-start(bf16[256,256]{1,0:T(8,128)(2,1)S(1)} %collective-permute-done.7.refs_3_), channel_id=1, source_target_pairs={{0,1},{1,0},{2,3},{3,2},{4,5},{5,4},{6,7},{7,6},{8,9},{9,8},{10,11... | collective-permute-start | bytes 393224 | tf_op jit(solution)/shard_map/ppermute | solution.py:173
  62.2 5.4 %collective-permute-start.10 = (bf16[256,256]{1,0:T(8,128)(2,1)S(1)}, bf16[256,256]{1,0:T(8,128)(2,1)S(1)}, u32[]{:S(2)}, u32[]{:S(2)}) collective-permute-start(bf16[256,256]{1,0:T(8,128)(2,1)S(1)} %collective-permute-done.6.refs_2_), channel_id=1, source_target_pairs={{0,1},{1,0},{2,3},{3,2},{4,5},{5,4},{6,7},{7,6},{8,9},{9,8},{10,11... | collective-permute-start | bytes 393224 | tf_op jit(solution)/shard_map/ppermute | solution.py:173
  64.9 3.7 %collective-permute-start.9 = (bf16[256,256]{1,0:T(8,128)(2,1)S(1)}, bf16[256,256]{1,0:T(8,128)(2,1)S(1)}, u32[]{:S(2)}, u32[]{:S(2)}) collective-permute-start(bf16[256,256]{1,0:T(8,128)(2,1)S(1)} %collective-permute-done.5.refs_1_), channel_id=1, source_target_pairs={{0,1},{1,0},{2,3},{3,2},{4,5},{5,4},{6,7},{7,6},{8,9},{9,8},{10,11... | collective-permute-start | bytes 393224 | tf_op jit(solution)/shard_map/ppermute | solution.py:173
